TPU v7x, 16 devices: a whole 2x2x2 slice. The times are simulated.
16 devices in a mesh: dp: 2 (over z), tp: 8 (over y, x, core).
Axes of the slice: x: 2, y: 2, z: 2, core: 2. Of those that a mesh axis runs over, the one named last changes fastest.
Arguments:
- hidden: bfloat16 [1024, 2560], P('dp'), parts along dimension 0
- norm_gain: float32 [2560], replicated
- emb_table: bfloat16 [32768, 2560], P('tp')
- teacher_ids: int32 [1024, 256], P('dp'), parts along dimension 0
- teacher_q: float32 [1024, 256], P('dp'), parts along dimension 0
Outputs:
- output 1: float32 [2], P('dp'), parts along dimension 0
- output 2: bfloat16 [1024, 2560], P('dp'), parts along dimension 0
- output 3: float32 [5120], P('dp'), parts along dimension 0
- output 4: float32 [65536, 2560], P(('dp', 'tp')), parts along dimension 0
There are 2 independent parts. A program takes and returns all parts, laid end to end along the dimension named above; an argument that names none is the same for every part.
All inputs are finite; a program needn't handle non-finite values.
Results may differ from a plain program's by a relative error of at most 0.001.
Values sent between devices are 32-bit elements.
A program may use at most 1 GiB of HBM per device.

v0:
```python
import jax
import jax.numpy as jnp
from jax import lax
from jax.sharding import PartitionSpec as P


def norm_apply(hid_f, gain_vec):
    inv_rms = lax.rsqrt(jnp.mean(hid_f * hid_f, axis=-1, keepdims=True) + 1e-6)
    return hid_f * inv_rms * (1.0 + gain_vec)


def solution(mesh):
    def local_step(hidden, norm_gain, emb_block, teacher_ids, teacher_q):
        tokens = hidden.shape[0]
        block_rows = emb_block.shape[0]
        block_start = lax.axis_index('tp') * block_rows
        normed, norm_pull = jax.vjp(norm_apply, hidden.astype(jnp.float32), norm_gain)
        x_in = normed.astype(jnp.bfloat16)
        logits = lax.dot_general(x_in, emb_block, (((1,), (1,)), ((), ())), preferred_element_type=jnp.float32)
        row_peak = lax.pmax(jnp.max(logits, axis=1), 'tp')
        exp_total = lax.psum(jnp.sum(jnp.exp(logits - row_peak[:, None]), axis=1), 'tp')
        log_z = row_peak + jnp.log(exp_total)
        local_ids = teacher_ids - block_start
        is_owned = (local_ids >= 0) & (local_ids < block_rows)
        safe_ids = jnp.clip(local_ids, 0, block_rows - 1)
        picked_local = jnp.where(is_owned, jnp.take_along_axis(logits, safe_ids, axis=1), 0.0)
        picked = lax.psum(picked_local, 'tp')
        q_total = jnp.sum(teacher_q, axis=1)
        token_loss = q_total * log_z - jnp.sum(teacher_q * picked, axis=1)
        mean_loss = jnp.mean(token_loss)[None]
        softmax_p = jnp.exp(logits - log_z[:, None])
        row_index = jnp.arange(tokens)[:, None]
        target_q = jnp.zeros_like(logits).at[row_index, safe_ids].add(jnp.where(is_owned, teacher_q, 0.0))
        grad_z = ((softmax_p * q_total[:, None] - target_q) / tokens).astype(jnp.bfloat16)
        grad_part = jnp.dot(grad_z, emb_block, preferred_element_type=jnp.float32)
        grad_x = lax.psum(grad_part, 'tp')
        grad_block = lax.dot_general(grad_z, x_in, (((0,), (0,)), ((), ())), preferred_element_type=jnp.float32)
        grad_h, grad_gain = norm_pull(grad_x)
        return (mean_loss, grad_h.astype(jnp.bfloat16), grad_gain, grad_block)

    return jax.shard_map(local_step, mesh=mesh, in_specs=(P('dp', None), P(None), P('tp', None), P('dp', None), P('dp', None)), out_specs=(P('dp'), P('dp', None), P('dp'), P(('dp', 'tp'), None)), check_vma=False)
```

profile of v0, /device:TPU:1, one launch (start us, length us, event | category | flops | bytes accessed | tf_op | source)
XLA Modules:
  0.0 6537.6 jit_solution(13064854674688819112)
XLA Ops:
  7.2 0.0 copy-start
  7.2 0.0 all-reduce.3.cloned.1.call-start
  7.2 2.5 fusion.5
  9.7 0.0 copy-start.9
  9.7 0.6 copy-done.9
  10.3 0.0 copy-start.11
  10.3 0.7 broadcast_add_fusion
  11.0 0.0 copy-start.7
  11.0 2.1 or_bitcast_fusion
  13.1 0.3 copy.9
  13.4 0.0 copy-done
  13.4 17.9 fusion.17
  31.3 0.0 copy-done.11
  31.3 0.0 copy-done.7
  31.3 0.0 copy-start.5
  31.3 0.0 copy-start.6
  31.3 0.0 copy-start.3
  31.3 0.0 copy-start.15
  31.4 3914.2 %gather_fusion = f32[131072]{0:T(1024)S(1)} fusion(f32[512,4096]{1,0:T(8,128)} %get-tuple-element.15, s32[131072]{0:T(1024)S(1)} %bitcast.18), kind=kCustom, calls=%fused_computation | custom fusion | bytes 2097152 | tf_op jit(solution)/shard_map/jit(take_along_axis)/gather | solution.py:26
  3945.6 0.0 copy-start.14
  3945.6 0.0 copy-start.13
  3945.6 0.1 reshape.50
  3945.8 0.0 copy-done.5
  3945.8 0.0 copy-done.6
  3945.8 1.1 select_bitcast_fusion.1
  3946.9 0.0 all-reduce.3.cloned.1.call-update
  3946.9 0.0 all-reduce.5.cloned.1.call-start
  3947.0 0.0 copy-done.3
  3947.0 0.0 copy-done.15
  3947.0 0.3 and_reduce_fusion
  3947.3 0.0 copy-done.14
  3947.3 0.1 multiply_reduce_fusion
  3947.4 0.1 select_bitcast_fusion
  3947.5 0.3 copy.10
  3947.8 0.0 copy-done.13
  3947.8 1566.3 %pmax.7 = f32[512]{0:T(512)S(1)} all-reduce(f32[512]{0:T(512)S(1)} %copy-done.13), channel_id=1, replica_groups=mesh['dp'=2,'tp'=8] {'tp'}, use_global_device_ids=true, to_apply=%region_3.0 | all-reduce | flops 512 | bytes 4096 | tf_op jit(solution)/shard_map/pmax | solution.py:20
  5514.2 0.3 copy.11
  5514.4 696.3 %scatter_custom_fusion = f32[2097152]{0:T(1024)} fusion(s32[131072]{0:T(1024)S(1)} %bitcast.19, f32[131072]{0:T(1024)S(1)} %bitcast.20, f32[]{:T(128)} %constant.12.clone.1), kind=kCustom, calls=%fused_computation.16 | custom fusion | flops 131072 | bytes 8388612
  6210.7 9.4 reshape.46
  6220.1 4.6 exponential_reduce_fusion
  6224.8 184.7 %psum.21 = f32[512]{0:T(512)S(1)} all-reduce(f32[512]{0:T(512)S(1)} %exponential_reduce_fusion), channel_id=1, replica_groups=mesh['dp'=2,'tp'=8] {'tp'}, use_global_device_ids=true, to_apply=%region_5.6 | all-reduce | flops 512 | bytes 4096 | tf_op jit(solution)/shard_map/psum | solution.py:21
  6409.4 0.0 all-reduce.3.cloned.1.call-done
  6409.4 1.3 fusion.15
  6410.7 0.6 subtract_reduce_fusion
  6411.3 7.1 multiply_convert_fusion
  6418.4 0.0 copy-start.4
  6418.4 2.1 copy-done.4
  6420.5 16.8 fusion.18
  6437.3 0.0 copy-start.1
  6437.3 0.0 copy-start.8
  6437.3 0.0 copy-start.12
  6437.3 0.0 all-reduce.5.cloned.1.call-update
  6438.1 0.9 copy-done.1
  6439.0 0.0 copy-done.8
  6439.0 0.0 copy-done.12
  6439.0 22.4 fusion.9
  6461.4 0.0 copy-start.10
  6461.4 60.4 all-reduce.5.cloned.1.call-done
  6521.9 0.0 copy-start.2
  6521.9 4.9 fusion.3
  6526.8 0.0 copy-done.10
  6526.8 0.0 copy-done.2
  6526.8 2.8 fusion.4
  (3 shorter events, 0.1 us)
Async XLA Ops:
  7.2 6.2 copy-start
  7.2 6402.3 %all-reduce.3.cloned.1.call-start = ((), (), s32[]{:S(2)}) async-start(), calls=%async_computation | async-start | bytes 1048576 | tf_op jit(solution)/shard_map/psum | solution.py:27
  9.7 0.6 copy-start.9
  10.3 21.0 copy-start.11
  11.0 20.3 copy-start.7
  31.3 3914.5 %copy-start.5 = (s32[512,256]{1,0:T(8,128)S(1)}, s32[512,256]{1,0:T(8,128)}, u32[]{:S(2)}) copy-start(s32[512,256]{1,0:T(8,128)} %param.8) | copy-start | bytes 1572868
  31.3 3914.5 %copy-start.6 = (f32[512,256]{1,0:T(8,128)S(1)}, f32[512,256]{1,0:T(8,128)}, u32[]{:S(2)}) copy-start(f32[512,256]{1,0:T(8,128)} %param.9) | copy-start | bytes 1572868
  31.3 3915.7 %copy-start.3 = (s32[512,256,1]{1,0,2:T(8,128)S(1)}, s32[512,256,1]{1,0,2:T(8,128)}, u32[]{:S(2)}) copy-start(s32[512,256,1]{1,0,2:T(8,128)} %get-tuple-element.11) | copy-start | bytes 1572868
  31.3 3915.7 %copy-start.15 = (s32[2]{0:T(128)S(1)}, s32[2]{0:T(128)}, u32[]{:S(2)}) copy-start(s32[2]{0:T(128)} %constant.51) | copy-start | bytes 28
  3945.6 1.7 copy-start.14
  3945.6 2.2 copy-start.13
  3946.9 2575.0 %all-reduce.5.cloned.1.call-start = ((), (), s32[]{:S(2)}) async-start(), calls=%async_computation.1 | async-start | bytes 10485760 | tf_op jit(solution)/shard_map/psum | solution.py:36
  6418.4 2.1 copy-start.4
  6437.3 1.8 copy-start.1
  6437.3 1.8 copy-start.8
  6437.3 1.8 copy-start.12
  6461.4 65.4 copy-start.10
  6521.9 4.9 copy-start.2
Sparse Core Ops, SparseCore 0:
  3947.0 1601.9 all-reduce.2
  6437.4 84.4 all-reduce.4
where the time goes:
time: 6640 us; the launch traced here: 6540 us
  local copies, waits for them, and re-layouts  3930 us (59%)
  blocking collectives  1750 us (26%)
  other arithmetic  724 us (11%)
    gather x3, local copies, waits for them, and re-layouts, local_step(): jnp.take_along_axis(logits, safe_ids, axis=1)  3910 us
    pmax x1, blocking collectives, local_step(): row_peak = lax.pmax(jnp.max(logits, axis=1), 'tp')  1570 us
    unnamed x6, other arithmetic  700 us
    psum x1, blocking collectives, local_step(): lax.psum(jnp.sum(jnp.exp(logits - row_peak[:, None]), axis=1), 'tp')  185 us
  transfers between devices with their start and end apart: 2, of which 1 were waited for; matrix products, arithmetic and copies ran while one was open for 11% of the time, Pallas kernels for 0%

commit v1 on v0

v1 whole, which is shorter than its diff:
```python
import jax
import jax.numpy as jnp
from jax import lax
from jax.experimental import pallas as pl
from jax.experimental.pallas import tpu as pltpu
from jax.sharding import PartitionSpec as P

MESH = pl.DeviceIdType.MESH
F32 = jnp.float32
BF16 = jnp.bfloat16
NT = (((1,), (1,)), ((), ()))
TN = (((0,), (0,)), ((), ()))
CHUNKS = 4
VT = 256


def fused_kernel(n_dev, h_hbm, w_ref, e_hbm, ids_hbm, q_hbm,
                 dh_hbm, dw_ref, loss_ref, dz_hbm, x_hbm,
                 h_v, x_v, e_v, ids_v, q_v, z_v, mx_v, sm_v, lz_v, sn_v, qs_v, dz_v, dx_v, dh_v, g_v,
                 r0_v, r1_v, r2_v, st_send, st_recv, fin_send, fin_recv, dwacc_v, qz_v,
                 e_sem, in_sem, out_sem, st_ss, st_rs, fin_ss, fin_rs, ss, rs):
    tokens, dim = h_v.shape
    vocab = e_v.shape[0]
    rows_c = tokens // CHUNKS
    groups = vocab // 128
    half = rows_c // 2
    n_blk = vocab // VT
    me = lax.axis_index('tp')
    dp = lax.axis_index('dp')
    core = me % 2
    xc = (me // 2) % 2
    yc = me // 4
    sib = me + 1 - 2 * core
    xn = me + 2 - 4 * xc
    yn = me + 4 - 8 * yc
    base = me * vocab
    inv_tokens = 1.0 / tokens

    def al(value, mult):
        return pl.multiple_of(value, mult)

    h_copy = pltpu.make_async_copy(h_hbm, h_v, in_sem.at[0])
    h_copy.start()

    def e_copy(i):
        rows = pl.ds(al(i * VT, VT), VT)
        return pltpu.make_async_copy(e_hbm.at[rows], e_v.at[rows], e_sem.at[i])

    @pl.loop(0, n_blk)
    def _(i):
        e_copy(i).start()

    ids_copy = pltpu.make_async_copy(ids_hbm, ids_v, in_sem.at[1])
    q_copy = pltpu.make_async_copy(q_hbm, q_v, in_sem.at[2])
    ids_copy.start()
    q_copy.start()

    barrier = pltpu.get_barrier_semaphore()
    for i in range(1, n_dev):
        pl.semaphore_signal(barrier, inc=1, device_id=(dp, (me + i) % n_dev), device_id_type=MESH)

    h_copy.wait()
    gain = w_ref[...] + 1.0

    @pl.loop(0, tokens // 16)
    def _(i):
        rows = pl.ds(al(i * 16, 16), 16)
        hf = h_v[rows, :].astype(F32)
        inv = lax.rsqrt(jnp.mean(hf * hf, axis=1, keepdims=True) + 1e-6)
        x_v[rows, :] = (hf * inv * gain).astype(BF16)

    x_copy = pltpu.make_async_copy(x_v, x_hbm, out_sem.at[0])
    x_copy.start()

    mx_v[...] = jnp.full(mx_v.shape, -jnp.inf, F32)

    @pl.loop(0, n_blk)
    def _(i):
        e_copy(i).wait()
        zb = lax.dot_general(x_v[...], e_v[pl.ds(al(i * VT, VT), VT), :], NT, preferred_element_type=F32)
        z_v[:, pl.ds(al(i * VT, VT), VT)] = zb
        top = zb[:, 0:128]
        for k in range(1, VT // 128):
            top = jnp.maximum(top, zb[:, 128 * k:128 * (k + 1)])
        mx_v[...] = jnp.maximum(mx_v[...], top)

    @pl.loop(0, tokens // 32)
    def _(i):
        rows = pl.ds(al(i * 32, 32), 32)
        peak = jnp.max(mx_v[rows, :], axis=1, keepdims=True)
        acc = jnp.zeros((32, 128), F32)
        for k in range(groups):
            acc = acc + jnp.exp(z_v[rows, 128 * k:128 * (k + 1)] - peak)
        mx_v[rows, :] = jnp.broadcast_to(peak, (32, 128))
        sm_v[rows, :] = jnp.broadcast_to(jnp.sum(acc, axis=1, keepdims=True), (32, 128))

    for b in range(tokens // 128):
        span = slice(128 * b, 128 * (b + 1))
        st_send[:, 128 * b:128 * (b + 1)] = mx_v[span, :].T[0:1, :]
        st_send[:, tokens + 128 * b:tokens + 128 * (b + 1)] = sm_v[span, :].T[0:1, :]
    st_recv[me] = st_send[...]

    pl.semaphore_wait(barrier, n_dev - 1)

    def gather_copies(src, dst, s_sem, r_sem):
        out = []
        for i in range(1, n_dev):
            out.append(pltpu.make_async_remote_copy(
                src_ref=src, dst_ref=dst.at[me], send_sem=s_sem.at[i - 1], recv_sem=r_sem.at[i - 1],
                device_id=(dp, (me + i) % n_dev), device_id_type=MESH))
        return out

    st_copies = gather_copies(st_send, st_recv, st_ss, st_rs)
    for copy in st_copies:
        copy.start()

    ids_copy.wait()
    q_copy.wait()

    iota_hi = lax.broadcasted_iota(jnp.int32, (groups, 256), 0)
    iota_lo = lax.broadcasted_iota(jnp.int32, (128, 256), 0)

    def build_q(c):
        @pl.loop(0, rows_c // 8)
        def _(t):
            for u in range(8):
                local = t * 8 + u
                row = pl.ds(c * rows_c + local, 1)
                ids = ids_v[row, :] - base
                qv = q_v[row, :]
                q_a = qv.astype(BF16).astype(F32)
                rest = qv - q_a
                q_b = rest.astype(BF16).astype(F32)
                q_c = rest - q_b
                hot_hi = lax.shift_right_arithmetic(ids, 7) == iota_hi
                hot_lo = jnp.where((ids & 127) == iota_lo, 1.0, 0.0).astype(BF16)
                parts = [jnp.where(hot_hi, part, 0.0).astype(BF16) for part in (q_a, q_b, q_c)]
                res = lax.dot_general(jnp.concatenate(parts, axis=0), hot_lo, NT, preferred_element_type=F32)
                dense = res[0:groups] + res[groups:2 * groups] + res[2 * groups:3 * groups]
                qs_v[pl.ds(local, groups, stride=rows_c), :] = dense

    def make_dz(c):
        @pl.loop(0, rows_c // 16)
        def _(i):
            off = al(i * 16, 16)
            rows = pl.ds(al(c * rows_c + off, 16), 16)
            lz = lz_v[rows, :]
            sn = sn_v[rows, :]
            acc = jnp.zeros((16, 128), F32)
            for k in range(groups):
                zz = z_v[rows, 128 * k:128 * (k + 1)]
                qq = qs_v[pl.ds(al(k * rows_c + off, 16), 16), :]
                acc = acc + qq * zz
                d = (jnp.exp(zz - lz) * sn - qq) * inv_tokens
                dz_v[rows, 128 * k:128 * (k + 1)] = d.astype(BF16)
            qz_v[...] = qz_v[...] + acc

    def make_dx(c):
        rows = slice(c * rows_c, (c + 1) * rows_c)

        @pl.loop(0, dim // 256)
        def _(j):
            cols = pl.ds(al(j * 256, 256), 256)
            dx_v[rows, cols] = jnp.dot(dz_v[rows, :], e_v[:, cols], preferred_element_type=F32)

    q8 = half // 8
    q4 = half // 4
    q2 = half // 2

    def rcopy(src, dst, c, slot, dev):
        return pltpu.make_async_remote_copy(
            src_ref=src, dst_ref=dst, send_sem=ss.at[c, slot], recv_sem=rs.at[c, slot],
            device_id=(dp, dev), device_id_type=MESH)

    def mine(c):
        return c * rows_c + half * core

    sent = []

    def go(*copies):
        for copy in copies:
            copy.start()
            sent.append(copy)

    def s0(c):
        return rcopy(dx_v.at[pl.ds(al(c * rows_c + half * (1 - core), half), half)], r0_v.at[c], c, 0, sib)

    def s1(c):
        a = rcopy(dx_v.at[pl.ds(al(mine(c) + q4 * (1 - xc), q4), q4)], r1_v.at[c, 0], c, 1, xn)
        b = rcopy(dx_v.at[pl.ds(al(mine(c) + q2 + q4 * (1 - yc), q4), q4)], r1_v.at[c, 1], c, 2, yn)
        return a, b

    def s2(c):
        a = rcopy(dx_v.at[pl.ds(al(mine(c) + q4 * xc + q8 * (1 - yc), q8), q8)], r2_v.at[c, 0], c, 3, yn)
        b = rcopy(dx_v.at[pl.ds(al(mine(c) + q2 + q4 * yc + q8 * (1 - xc), q8), q8)], r2_v.at[c, 1], c, 4, xn)
        return a, b

    def s3(c):
        rows_a = pl.ds(al(mine(c) + q4 * xc + q8 * yc, q8), q8)
        rows_b = pl.ds(al(mine(c) + q2 + q4 * yc + q8 * xc, q8), q8)
        return (rcopy(g_v.at[rows_a], g_v.at[rows_a], c, 5, yn), rcopy(g_v.at[rows_b], g_v.at[rows_b], c, 6, xn))

    def s4(c):
        rows_a = pl.ds(al(mine(c) + q4 * xc, q4), q4)
        rows_b = pl.ds(al(mine(c) + q2 + q4 * yc, q4), q4)
        return (rcopy(g_v.at[rows_a], g_v.at[rows_a], c, 7, xn), rcopy(g_v.at[rows_b], g_v.at[rows_b], c, 8, yn))

    def s5(c):
        rows = pl.ds(al(mine(c), half), half)
        return rcopy(g_v.at[rows], g_v.at[rows], c, 9, sib)

    def f0(c):
        go(s0(c))

    def f1(c):
        s0(c).wait_recv()

        @pl.loop(0, half // 8)
        def _(i):
            rows = pl.ds(al(mine(c) + 8 * i, 8), 8)
            dx_v[rows, :] = dx_v[rows, :] + r0_v[c, pl.ds(al(8 * i, 8), 8), :]
        go(*s1(c))

    def f2(c):
        a, b = s1(c)
        a.wait_recv()
        b.wait_recv()
        for k, start in ((0, mine(c) + q4 * xc), (1, mine(c) + q2 + q4 * yc)):
            rows = pl.ds(al(start, q4), q4)
            dx_v[rows, :] = dx_v[rows, :] + r1_v[c, k]
        go(*s2(c))

    def norm_back(c, k, block, side):
        rows16 = pl.ds(al(block, 16), 16)
        rows = pl.ds(al(block + q8 * side, q8), q8)
        hb = h_v[rows16, :].astype(F32)
        hf = jnp.where(side == 0, hb[0:8, :], hb[8:16, :])
        grad = dx_v[rows, :] + r2_v[c, k]
        inv = lax.rsqrt(jnp.mean(hf * hf, axis=1, keepdims=True) + 1e-6)
        scaled = grad * gain
        mean = jnp.sum(scaled * hf, axis=1, keepdims=True) * (1.0 / dim)
        g_v[rows, :] = scaled * inv - hf * (inv * inv * inv * mean)
        dwacc_v[...] = dwacc_v[...] + grad * hf * inv

    def f3(c):
        a, b = s2(c)
        a.wait_recv()
        b.wait_recv()
        norm_back(c, 0, mine(c) + q4 * xc, yc)
        norm_back(c, 1, mine(c) + q2 + q4 * yc, xc)
        go(*s3(c))

    def f4(c):
        a, b = s3(c)
        a.wait_recv()
        b.wait_recv()
        go(*s4(c))

    def f5(c):
        a, b = s4(c)
        a.wait_recv()
        b.wait_recv()
        go(s5(c))

    def rows_of(c):
        return slice(c * rows_c, (c + 1) * rows_c)

    def dh_copy(c):
        return pltpu.make_async_copy(dh_v.at[rows_of(c)], dh_hbm.at[rows_of(c)], out_sem.at[1 + c])

    def dz_copy(c):
        return pltpu.make_async_copy(dz_v.at[rows_of(c)], dz_hbm.at[rows_of(c)], out_sem.at[1 + CHUNKS + c])

    def f6(c):
        s5(c).wait_recv()

        @pl.loop(0, rows_c // 16)
        def _(i):
            rows = pl.ds(al(c * rows_c + 16 * i, 16), 16)
            dh_v[rows, :] = g_v[rows, :].astype(BF16)
        dh_copy(c).start()

    dwacc_v[...] = jnp.zeros(dwacc_v.shape, F32)
    qz_v[...] = jnp.zeros(qz_v.shape, F32)
    build_q(0)

    @pl.loop(0, tokens // 16)
    def _(i):
        rows = pl.ds(al(i * 16, 16), 16)
        sn_v[rows, :] = jnp.broadcast_to(jnp.sum(q_v[rows, :], axis=1, keepdims=True), (16, 128))

    for copy in st_copies:
        copy.wait_recv()
    peak = st_recv[0][:, 0:tokens]
    for d in range(1, n_dev):
        peak = jnp.maximum(peak, st_recv[d][:, 0:tokens])
    total = jnp.zeros((1, tokens), F32)
    for d in range(n_dev):
        total = total + st_recv[d][:, tokens:2 * tokens] * jnp.exp(st_recv[d][:, 0:tokens] - peak)
    log_z = peak + jnp.log(total)
    for b in range(tokens // 128):
        lz_v[128 * b:128 * (b + 1), :] = jnp.broadcast_to(log_z[:, 128 * b:128 * (b + 1)], (128, 128)).T

    def chunk(c):
        make_dz(c)
        dz_copy(c).start()
        make_dx(c)

    chunk(0)
    f0(0)
    build_q(1)
    f1(0)
    chunk(1)
    f0(1)
    f2(0)
    build_q(2)
    f1(1)
    f3(0)
    chunk(2)
    f0(2)
    f2(1)
    f4(0)
    build_q(3)
    f1(2)
    f3(1)
    f5(0)
    chunk(3)
    f0(3)
    f2(2)
    f4(1)
    f6(0)
    f1(3)
    f3(2)
    f5(1)
    f2(3)
    f4(2)
    f6(1)
    f3(3)
    fin_send[:, 0:dim] = jnp.sum(dwacc_v[...], axis=0, keepdims=True)
    fin_send[:, dim:dim + 128] = jnp.sum(qz_v[...], axis=0, keepdims=True)
    fin_recv[me] = fin_send[...]
    fin_copies = gather_copies(fin_send, fin_recv, fin_ss, fin_rs)
    for copy in fin_copies:
        copy.start()
    f5(2)
    f4(3)
    f6(2)
    f5(3)

    for copy in fin_copies:
        copy.wait_recv()
    fin = fin_recv[0]
    for d in range(1, n_dev):
        fin = fin + fin_recv[d]
    dw_ref[...] = fin[:, 0:dim]
    weighted = jnp.sum(lz_v[...] * sn_v[...], axis=0, keepdims=True)
    loss_ref[...] = (weighted - jnp.sum(fin[:, dim:dim + 128])) * inv_tokens
    f6(3)

    for copy in st_copies + sent + fin_copies:
        copy.wait_send()
    x_copy.wait()
    for c in range(CHUNKS):
        dz_copy(c).wait()
        dh_copy(c).wait()


def table_kernel(dz_ref, x_ref, out_ref):
    out_ref[...] = lax.dot_general(dz_ref[...], x_ref[...], TN, preferred_element_type=F32)


def solution(mesh):
    n_dev = mesh.shape['tp']

    def local_step(hidden, norm_gain, emb_block, teacher_ids, teacher_q):
        tokens, dim = hidden.shape
        vocab = emb_block.shape[0]
        rows_c = tokens // CHUNKS
        half = rows_c // 2
        kt = teacher_ids.shape[1]
        any_spec = pl.BlockSpec(memory_space=pl.ANY)
        vmem_spec = pl.BlockSpec(memory_space=pltpu.VMEM)
        vm = pltpu.VMEM
        dma = pltpu.SemaphoreType.DMA
        dh, dw, loss, dz, x_in = pl.pallas_call(
            lambda *refs: fused_kernel(n_dev, *refs),
            out_shape=(
                jax.ShapeDtypeStruct((tokens, dim), BF16),
                jax.ShapeDtypeStruct((1, dim), F32),
                jax.ShapeDtypeStruct((1, 128), F32),
                jax.ShapeDtypeStruct((tokens, vocab), BF16),
                jax.ShapeDtypeStruct((tokens, dim), BF16),
            ),
            in_specs=[any_spec, vmem_spec, any_spec, any_spec, any_spec],
            out_specs=(any_spec, vmem_spec, vmem_spec, any_spec, any_spec),
            scratch_shapes=[
                vm((tokens, dim), BF16),
                vm((tokens, dim), BF16),
                vm((vocab, dim), BF16),
                vm((tokens, kt), jnp.int32),
                vm((tokens, kt), F32),
                vm((tokens, vocab), F32),
                vm((tokens, 128), F32),
                vm((tokens, 128), F32),
                vm((tokens, 128), F32),
                vm((tokens, 128), F32),
                vm((vocab // 128 * rows_c, 128), F32),
                vm((tokens, vocab), BF16),
                vm((tokens, dim), F32),
                vm((tokens, dim), BF16),
                vm((tokens, dim), F32),
                vm((CHUNKS, half, dim), F32),
                vm((CHUNKS, 2, half // 4, dim), F32),
                vm((CHUNKS, 2, half // 8, dim), F32),
                vm((1, 2 * tokens), F32),
                vm((n_dev, 1, 2 * tokens), F32),
                vm((1, dim + 128), F32),
                vm((n_dev, 1, dim + 128), F32),
                vm((8, dim), F32),
                vm((16, 128), F32),
                dma((vocab // VT,)),
                dma((3,)),
                dma((1 + 2 * CHUNKS,)),
                dma((n_dev - 1,)),
                dma((n_dev - 1,)),
                dma((n_dev - 1,)),
                dma((n_dev - 1,)),
                dma((CHUNKS, 10)),
                dma((CHUNKS, 10)),
            ],
            compiler_params=pltpu.CompilerParams(
                collective_id=0, has_side_effects=True, vmem_limit_bytes=67_043_328),
            name='fused_head',
        )(hidden, norm_gain[None, :], emb_block, teacher_ids, teacher_q)
        grad_block = pl.pallas_call(
            table_kernel,
            grid=(vocab // VT,),
            in_specs=[pl.BlockSpec((tokens, VT), lambda i: (0, i)), pl.BlockSpec((tokens, dim), lambda i: (0, 0))],
            out_specs=pl.BlockSpec((VT, dim), lambda i: (i, 0)),
            out_shape=jax.ShapeDtypeStruct((vocab, dim), F32),
            name='table_grad',
        )(dz, x_in)
        return (loss[0, 0:1], dh, dw[0], grad_block)

    return jax.shard_map(local_step, mesh=mesh, in_specs=(P('dp', None), P(None), P('tp', None), P('dp', None), P('dp', None)), out_specs=(P('dp'), P('dp', None), P('dp'), P(('dp', 'tp'), None)), check_vma=False)
```

time: 6640 us -> 130 us (0.02); the launches traced: 6540 us -> 129 us
  local copies, waits for them, and re-layouts: 3930 us -> 2.82 us
  blocking collectives: 1750 us -> 0 us
  other arithmetic: 724 us -> 0.63 us
  Pallas kernels: 0 us -> 124 us
    gather x3 -> x0, local copies, waits for them, and re-layouts: 3910 us -> none  [local_step(): jnp.take_along_axis(logits, safe_ids, axis=1)]
    pmax x1 -> x0, blocking collectives: 1570 us -> none  [local_step(): row_peak = lax.pmax(jnp.max(logits, axis=1), 'tp')]
    unnamed x6 -> x0, other arithmetic: 700 us -> none
    psum x1 -> x0, blocking collectives: 185 us -> none  [local_step(): lax.psum(jnp.sum(jnp.exp(logits - row_peak[:, None]), axis=1), 'tp')]
    pallas_call x0 -> x2, Pallas kernels: none -> 124 us  [the longest x1 102 us: local_step(): pl.pallas_call(lambda *refs: fused_kernel(n_dev, *refs), out_shape=(jax.S...]
  transfers between devices with their start and end apart: 2 -> 0, of which waited for: 1 -> 0; matrix products, arithmetic and copies ran while one was open for 11% -> 0% of each run, Pallas kernels for 0% -> 0%
where the time goes in v1:
time: 130 us; the launch traced here: 129 us
  Pallas kernels  124 us (95%)
  local copies, waits for them, and re-layouts  2.82 us (2%)
  between operations  1.84 us (1%)
    pallas_call x1, Pallas kernels, local_step(): pl.pallas_call(lambda *refs: fused_kernel(n_dev, *refs), out_shape=(jax.S...  102 us
    pallas_call x1, Pallas kernels, local_step(): pl.pallas_call(table_kernel, grid=(vocab // VT,), in_specs=[pl.BlockSpec(...  22 us

profile of v1, /device:TPU:1, one launch (start us, length us, event | category | flops | bytes accessed | tf_op | source)
XLA Modules:
  0.0 129.0 jit_solution(2858322749213468784)
XLA Ops:
  0.6 1.3 %broadcast_in_dim.3.refs_1_ = f32[1,2560]{1,0:T(1,128)} reshape(f32[2560]{0:T(1024)} %param.6) | data formatting | bytes 20480 | tf_op jit(solution)/shard_map/broadcast_in_dim | solution.py:434
  1.9 101.7 %fused_head.1 = (bf16[512,2560]{1,0:T(8,128)(2,1)}, f32[1,2560]{1,0:T(1,128)}, f32[1,128]{1,0:T(1,128)}, bf16[512,4096]{1,0:T(8,128)(2,1)}, bf16[512,2560]{1,0:T(8,128)(2,1)}) custom-call(bf16[512,2560]{1,0:T(8,128)(2,1)} %refs_0_.1, f32[1,2560]{1,0:T(1,128)} %broadcast_in_dim.3.refs_1_, bf16[4096,2560]{1,0:T(8,128)(2,1)} %refs_2_.1, s32[512,256]{1,0:T(8,128)} %refs_3_.1, ...), custom_call_target="tpu_custom_call" | custom-call | tf_op jit(solution)/shard_map/fused_head/pallas_call | solution.py:385
  103.6 0.0 copy-start.1
  103.7 0.0 copy-start.2
  103.7 0.0 copy-start
  103.7 22.0 %table_grad.1 = f32[4096,2560]{1,0:T(8,128)} custom-call(bf16[512,4096]{1,0:T(8,128)(2,1)} %get-tuple-element.12.dz_ref, bf16[512,2560]{1,0:T(8,128)(2,1)} %get-tuple-element.13.x_ref), custom_call_target="tpu_custom_call" | custom-call | tf_op jit(solution)/shard_map/table_grad/pallas_call | solution.py:435
  125.7 0.0 copy-done.1
  125.7 0.6 reduce
  126.3 0.0 copy-done.2
  126.4 0.0 copy-done
  126.4 1.5 %copy.12 = bf16[512,2560]{1,0:T(8,128)(2,1)} copy(bf16[512,2560]{1,0:T(8,128)(2,1)S(1)} %copy-done) | data formatting | bytes 5242880
Async XLA Ops:
  103.6 22.0 %copy-start.1 = (f32[1,2560]{1,0:T(1,128)S(1)}, f32[1,2560]{1,0:T(1,128)}, u32[]{:S(2)}) copy-start(f32[1,2560]{1,0:T(1,128)} %get-tuple-element.11) | copy-start | bytes 30724
  103.7 22.7 %copy-start.2 = (f32[1,128]{1,0:T(1,128)S(1)}, f32[1,128]{1,0:T(1,128)}, u32[]{:S(2)}) copy-start(f32[1,128]{1,0:T(1,128)} %get-tuple-element.9) | copy-start | bytes 1540
  103.7 22.7 %copy-start = (bf16[512,2560]{1,0:T(8,128)(2,1)S(1)}, bf16[512,2560]{1,0:T(8,128)(2,1)}, u32[]{:S(2)}) copy-start(bf16[512,2560]{1,0:T(8,128)(2,1)} %get-tuple-element.19) | copy-start | bytes 7864324

commit v2 on v1

--- a/solution.py
+++ b/solution.py
@@ -12,6 +12,7 @@
 TN = (((0,), (0,)), ((), ()))
 CHUNKS = 4
 VT = 256
+SLOTS = 4
 
 
 def fused_kernel(n_dev, h_hbm, w_ref, e_hbm, ids_hbm, q_hbm,
@@ -40,6 +41,9 @@
         return pl.multiple_of(value, mult)
 
     h_copy = pltpu.make_async_copy(h_hbm, h_v, in_sem.at[0])
+    ids_copy = pltpu.make_async_copy(ids_hbm, ids_v, in_sem.at[1])
+    q_copy = pltpu.make_async_copy(q_hbm, q_v, in_sem.at[2])
+    q_copy.start()
     h_copy.start()
 
     def e_copy(i):
@@ -50,54 +54,63 @@
     def _(i):
         e_copy(i).start()
 
-    ids_copy = pltpu.make_async_copy(ids_hbm, ids_v, in_sem.at[1])
-    q_copy = pltpu.make_async_copy(q_hbm, q_v, in_sem.at[2])
     ids_copy.start()
-    q_copy.start()
 
     barrier = pltpu.get_barrier_semaphore()
     for i in range(1, n_dev):
         pl.semaphore_signal(barrier, inc=1, device_id=(dp, (me + i) % n_dev), device_id_type=MESH)
 
+    q_copy.wait()
+
+    @pl.loop(0, tokens // 64)
+    def _(i):
+        rows = pl.ds(al(i * 64, 64), 64)
+        sn_v[rows, :] = jnp.broadcast_to(jnp.sum(q_v[rows, :], axis=1, keepdims=True), (64, 128))
+
     h_copy.wait()
-    gain = w_ref[...] + 1.0
-
-    @pl.loop(0, tokens // 16)
-    def _(i):
-        rows = pl.ds(al(i * 16, 16), 16)
-        hf = h_v[rows, :].astype(F32)
-        inv = lax.rsqrt(jnp.mean(hf * hf, axis=1, keepdims=True) + 1e-6)
-        x_v[rows, :] = (hf * inv * gain).astype(BF16)
+    gain = w_ref[...].reshape(1, dim) + 1.0
+
+    @pl.loop(0, tokens // 64)
+    def _(i):
+        rows = pl.ds(al(i * 64, 64), 64)
+        acc = jnp.zeros((64, 128), F32)
+        for k in range(dim // 128):
+            hf = h_v[rows, 128 * k:128 * (k + 1)].astype(F32)
+            acc = acc + hf * hf
+        inv = lax.rsqrt(jnp.sum(acc, axis=1, keepdims=True) * (1.0 / dim) + 1e-6)
+        inv = jnp.broadcast_to(inv, (64, 128))
+        for k in range(dim // 128):
+            hf = h_v[rows, 128 * k:128 * (k + 1)].astype(F32)
+            x_v[rows, 128 * k:128 * (k + 1)] = (hf * inv * gain[:, 128 * k:128 * (k + 1)]).astype(BF16)
 
     x_copy = pltpu.make_async_copy(x_v, x_hbm, out_sem.at[0])
     x_copy.start()
 
     mx_v[...] = jnp.full(mx_v.shape, -jnp.inf, F32)
+    sm_v[...] = jnp.zeros(sm_v.shape, F32)
 
     @pl.loop(0, n_blk)
     def _(i):
         e_copy(i).wait()
         zb = lax.dot_general(x_v[...], e_v[pl.ds(al(i * VT, VT), VT), :], NT, preferred_element_type=F32)
         z_v[:, pl.ds(al(i * VT, VT), VT)] = zb
-        top = zb[:, 0:128]
-        for k in range(1, VT // 128):
-            top = jnp.maximum(top, zb[:, 128 * k:128 * (k + 1)])
-        mx_v[...] = jnp.maximum(mx_v[...], top)
-
-    @pl.loop(0, tokens // 32)
-    def _(i):
-        rows = pl.ds(al(i * 32, 32), 32)
-        peak = jnp.max(mx_v[rows, :], axis=1, keepdims=True)
-        acc = jnp.zeros((32, 128), F32)
-        for k in range(groups):
-            acc = acc + jnp.exp(z_v[rows, 128 * k:128 * (k + 1)] - peak)
-        mx_v[rows, :] = jnp.broadcast_to(peak, (32, 128))
-        sm_v[rows, :] = jnp.broadcast_to(jnp.sum(acc, axis=1, keepdims=True), (32, 128))
+        old = mx_v[...]
+        new = old
+        for k in range(VT // 128):
+            new = jnp.maximum(new, zb[:, 128 * k:128 * (k + 1)])
+        total = sm_v[...] * jnp.exp(old - new)
+        for k in range(VT // 128):
+            total = total + jnp.exp(zb[:, 128 * k:128 * (k + 1)] - new)
+        mx_v[...] = new
+        sm_v[...] = total
 
     for b in range(tokens // 128):
         span = slice(128 * b, 128 * (b + 1))
-        st_send[:, 128 * b:128 * (b + 1)] = mx_v[span, :].T[0:1, :]
-        st_send[:, tokens + 128 * b:tokens + 128 * (b + 1)] = sm_v[span, :].T[0:1, :]
+        peaks = mx_v[span, :].T
+        peak = jnp.max(peaks, axis=0, keepdims=True)
+        st_send[:, 128 * b:128 * (b + 1)] = peak
+        st_send[:, tokens + 128 * b:tokens + 128 * (b + 1)] = jnp.sum(
+            sm_v[span, :].T * jnp.exp(peaks - peak), axis=0, keepdims=True)
     st_recv[me] = st_send[...]
 
     pl.semaphore_wait(barrier, n_dev - 1)
@@ -115,7 +128,6 @@
         copy.start()
 
     ids_copy.wait()
-    q_copy.wait()
 
     iota_hi = lax.broadcasted_iota(jnp.int32, (groups, 256), 0)
     iota_lo = lax.broadcasted_iota(jnp.int32, (128, 256), 0)
@@ -283,11 +295,6 @@
     dwacc_v[...] = jnp.zeros(dwacc_v.shape, F32)
     qz_v[...] = jnp.zeros(qz_v.shape, F32)
     build_q(0)
-
-    @pl.loop(0, tokens // 16)
-    def _(i):
-        rows = pl.ds(al(i * 16, 16), 16)
-        sn_v[rows, :] = jnp.broadcast_to(jnp.sum(q_v[rows, :], axis=1, keepdims=True), (16, 128))
 
     for copy in st_copies:
         copy.wait_recv()
@@ -352,7 +359,7 @@
     fin = fin_recv[0]
     for d in range(1, n_dev):
         fin = fin + fin_recv[d]
-    dw_ref[...] = fin[:, 0:dim]
+    dw_ref[...] = fin[:, 0:dim].reshape(dim)
     weighted = jnp.sum(lz_v[...] * sn_v[...], axis=0, keepdims=True)
     loss_ref[...] = (weighted - jnp.sum(fin[:, dim:dim + 128])) * inv_tokens
     f6(3)
@@ -365,8 +372,40 @@
         dh_copy(c).wait()
 
 
-def table_kernel(dz_ref, x_ref, out_ref):
-    out_ref[...] = lax.dot_general(dz_ref[...], x_ref[...], TN, preferred_element_type=F32)
+def table_kernel(dz_hbm, x_hbm, out_hbm, dz_v, x_v, o_v, x_sem, dz_sem, out_sem):
+    n_blk = out_hbm.shape[0] // VT
+
+    def dz_copy(i):
+        cols = pl.ds(pl.multiple_of(i * VT, VT), VT)
+        return pltpu.make_async_copy(dz_hbm.at[:, cols], dz_v.at[:, cols], dz_sem.at[i])
+
+    def out_copy(i):
+        slot = lax.rem(i, SLOTS)
+        return pltpu.make_async_copy(o_v.at[slot], out_hbm.at[pl.ds(pl.multiple_of(i * VT, VT), VT)], out_sem.at[slot])
+
+    x_copy = pltpu.make_async_copy(x_hbm, x_v, x_sem)
+    x_copy.start()
+
+    @pl.loop(0, n_blk)
+    def _(i):
+        dz_copy(i).start()
+
+    x_copy.wait()
+
+    @pl.loop(0, n_blk)
+    def _(i):
+        dz_copy(i).wait()
+
+        @pl.when(i >= SLOTS)
+        def _():
+            out_copy(i - SLOTS).wait()
+
+        o_v[lax.rem(i, SLOTS)] = lax.dot_general(
+            dz_v[:, pl.ds(pl.multiple_of(i * VT, VT), VT)], x_v[...], TN, preferred_element_type=F32)
+        out_copy(i).start()
+
+    for i in range(n_blk - SLOTS, n_blk):
+        out_copy(i).wait()
 
 
 def solution(mesh):
@@ -386,7 +425,7 @@
             lambda *refs: fused_kernel(n_dev, *refs),
             out_shape=(
                 jax.ShapeDtypeStruct((tokens, dim), BF16),
-                jax.ShapeDtypeStruct((1, dim), F32),
+                jax.ShapeDtypeStruct((dim,), F32),
                 jax.ShapeDtypeStruct((1, 128), F32),
                 jax.ShapeDtypeStruct((tokens, vocab), BF16),
                 jax.ShapeDtypeStruct((tokens, dim), BF16),
@@ -431,15 +470,23 @@
             compiler_params=pltpu.CompilerParams(
                 collective_id=0, has_side_effects=True, vmem_limit_bytes=67_043_328),
             name='fused_head',
-        )(hidden, norm_gain[None, :], emb_block, teacher_ids, teacher_q)
+        )(hidden, norm_gain, emb_block, teacher_ids, teacher_q)
         grad_block = pl.pallas_call(
             table_kernel,
-            grid=(vocab // VT,),
-            in_specs=[pl.BlockSpec((tokens, VT), lambda i: (0, i)), pl.BlockSpec((tokens, dim), lambda i: (0, 0))],
-            out_specs=pl.BlockSpec((VT, dim), lambda i: (i, 0)),
+            in_specs=[any_spec, any_spec],
+            out_specs=any_spec,
             out_shape=jax.ShapeDtypeStruct((vocab, dim), F32),
+            scratch_shapes=[
+                vm((tokens, vocab), BF16),
+                vm((tokens, dim), BF16),
+                vm((SLOTS, VT, dim), F32),
+                dma,
+                dma((vocab // VT,)),
+                dma((SLOTS,)),
+            ],
+            compiler_params=pltpu.CompilerParams(vmem_limit_bytes=67_043_328),
             name='table_grad',
         )(dz, x_in)
-        return (loss[0, 0:1], dh, dw[0], grad_block)
+        return (loss[0, 0:1], dh, dw, grad_block)
 
     return jax.shard_map(local_step, mesh=mesh, in_specs=(P('dp', None), P(None), P('tp', None), P('dp', None), P('dp', None)), out_specs=(P('dp'), P('dp', None), P('dp'), P(('dp', 'tp'), None)), check_vma=False)

time: 130 us -> 118 us (0.908)
  Pallas kernels: 124 us -> 111 us
    pallas_call x1, Pallas kernels: 102 us -> 93.2 us  [local_step(): pl.pallas_call(lambda *refs: fused_kernel(n_dev, *refs), out_shape=(jax.S...]
    pallas_call x1, Pallas kernels: 22 us -> 17.6 us  [local_step(): pl.pallas_call(table_kernel, in_specs=[any_spec, any_spec], out_specs=any...]
    unnamed x7 -> x4, local copies, waits for them, and re-layouts: 1.51 us -> 4.01 us
    broadcast_in_dim x1 -> x0, local copies, waits for them, and re-layouts: 1.31 us -> none  [local_step(): norm_gain[None, :]]
where the time goes in v2:
time: 118 us; the launch traced here: 117 us
  Pallas kernels  111 us (94%)
  local copies, waits for them, and re-layouts  4.01 us (3%)
  between operations  2.46 us (2%)
    pallas_call x1, Pallas kernels, local_step(): pl.pallas_call(lambda *refs: fused_kernel(n_dev, *refs), out_shape=(jax.S...  93.2 us
    pallas_call x1, Pallas kernels, local_step(): pl.pallas_call(table_kernel, in_specs=[any_spec, any_spec], out_specs=any...  17.6 us
    unnamed x4, local copies, waits for them, and re-layouts  4.01 us

profile of v2, /device:TPU:1, one launch (start us, length us, event | category | flops | bytes accessed | tf_op | source)
XLA Modules:
  0.0 117.3 jit_solution(7750280357682677099)
XLA Ops:
  0.6 93.2 %fused_head.1 = (bf16[512,2560]{1,0:T(8,128)(2,1)}, f32[2560]{0:T(1024)}, f32[1,128]{1,0:T(1,128)}, bf16[512,4096]{1,0:T(8,128)(2,1)}, bf16[512,2560]{1,0:T(8,128)(2,1)}) custom-call(bf16[512,2560]{1,0:T(8,128)(2,1)} %refs_0_.1, f32[2560]{0:T(1024)} %refs_1_.1, bf16[4096,2560]{1,0:T(8,128)(2,1)} %refs_2_.1, s32[512,256]{1,0:T(8,128)} %refs_3_.1, ...), custom_call_target="tpu_custom_call" | custom-call | tf_op jit(solution)/shard_map/fused_head/pallas_call | solution.py:424
  93.9 17.6 %table_grad.1 = f32[4096,2560]{1,0:T(8,128)} custom-call(bf16[512,4096]{1,0:T(8,128)(2,1)} %get-tuple-element.12.dz_hbm, bf16[512,2560]{1,0:T(8,128)(2,1)} %get-tuple-element.13.x_hbm), custom_call_target="tpu_custom_call" | custom-call | tf_op jit(solution)/shard_map/table_grad/pallas_call | solution.py:474
  112.1 0.0 copy-start
  112.1 3.4 %copy.13 = bf16[512,2560]{1,0:T(8,128)(2,1)} copy(bf16[512,2560]{1,0:T(8,128)(2,1)} %get-tuple-element.19) | data formatting | bytes 5242880
  115.5 0.0 copy-done
  115.6 0.6 copy.14
Async XLA Ops:
  112.1 3.4 %copy-start = (f32[2560]{0:T(1024)S(1)}, f32[2560]{0:T(1024)}, u32[]{:S(2)}) copy-start(f32[2560]{0:T(1024)} %get-tuple-element.20) | copy-start | bytes 30724

commit v3 on v2

--- a/solution.py
+++ b/solution.py
@@ -12,7 +12,9 @@
 TN = (((0,), (0,)), ((), ()))
 CHUNKS = 4
 VT = 256
-SLOTS = 4
+SLOTS = 3
+TT = 512
+TOK = 32
 
 
 def fused_kernel(n_dev, h_hbm, w_ref, e_hbm, ids_hbm, q_hbm,
@@ -133,10 +135,10 @@
     iota_lo = lax.broadcasted_iota(jnp.int32, (128, 256), 0)
 
     def build_q(c):
-        @pl.loop(0, rows_c // 8)
+        @pl.loop(0, rows_c // TOK)
         def _(t):
-            for u in range(8):
-                local = t * 8 + u
+            for u in range(TOK):
+                local = t * TOK + u
                 row = pl.ds(c * rows_c + local, 1)
                 ids = ids_v[row, :] - base
                 qv = q_v[row, :]
@@ -372,16 +374,20 @@
         dh_copy(c).wait()
 
 
-def table_kernel(dz_hbm, x_hbm, out_hbm, dz_v, x_v, o_v, x_sem, dz_sem, out_sem):
-    n_blk = out_hbm.shape[0] // VT
+def table_kernel(dz_hbm, x_hbm, dh_hbm, dw_ref, loss_ref, out_hbm, dh_out, dw_out, loss_out,
+                 dz_v, x_v, o_v, dh_v, x_sem, dz_sem, out_sem, dh_sem):
+    n_blk = out_hbm.shape[0] // TT
+    half = out_hbm.shape[1] // 2
+    cuts = (slice(0, half), slice(half, 2 * half))
 
     def dz_copy(i):
-        cols = pl.ds(pl.multiple_of(i * VT, VT), VT)
+        cols = pl.ds(pl.multiple_of(i * TT, TT), TT)
         return pltpu.make_async_copy(dz_hbm.at[:, cols], dz_v.at[:, cols], dz_sem.at[i])
 
-    def out_copy(i):
+    def out_copy(i, k):
         slot = lax.rem(i, SLOTS)
-        return pltpu.make_async_copy(o_v.at[slot], out_hbm.at[pl.ds(pl.multiple_of(i * VT, VT), VT)], out_sem.at[slot])
+        rows = pl.ds(pl.multiple_of(i * TT, TT), TT)
+        return pltpu.make_async_copy(o_v.at[slot, :, cuts[k]], out_hbm.at[rows, cuts[k]], out_sem.at[slot, k])
 
     x_copy = pltpu.make_async_copy(x_hbm, x_v, x_sem)
     x_copy.start()
@@ -390,6 +396,11 @@
     def _(i):
         dz_copy(i).start()
 
+    dh_in = pltpu.make_async_copy(dh_hbm, dh_v, dh_sem.at[0])
+    dh_put = pltpu.make_async_copy(dh_v, dh_out, dh_sem.at[1])
+    dh_in.start()
+    dw_out[...] = dw_ref[...]
+    loss_out[...] = loss_ref[...]
     x_copy.wait()
 
     @pl.loop(0, n_blk)
@@ -398,14 +409,24 @@
 
         @pl.when(i >= SLOTS)
         def _():
-            out_copy(i - SLOTS).wait()
-
-        o_v[lax.rem(i, SLOTS)] = lax.dot_general(
-            dz_v[:, pl.ds(pl.multiple_of(i * VT, VT), VT)], x_v[...], TN, preferred_element_type=F32)
-        out_copy(i).start()
+            out_copy(i - SLOTS, 0).wait()
+            out_copy(i - SLOTS, 1).wait()
+
+        cols = pl.ds(pl.multiple_of(i * TT, TT), TT)
+        for k in range(2):
+            o_v[lax.rem(i, SLOTS), :, cuts[k]] = lax.dot_general(
+                dz_v[:, cols], x_v[:, cuts[k]], TN, preferred_element_type=F32)
+            out_copy(i, k).start()
+
+        @pl.when(i == 1)
+        def _():
+            dh_in.wait()
+            dh_put.start()
 
     for i in range(n_blk - SLOTS, n_blk):
-        out_copy(i).wait()
+        out_copy(i, 0).wait()
+        out_copy(i, 1).wait()
+    dh_put.wait()
 
 
 def solution(mesh):
@@ -471,22 +492,29 @@
                 collective_id=0, has_side_effects=True, vmem_limit_bytes=67_043_328),
             name='fused_head',
         )(hidden, norm_gain, emb_block, teacher_ids, teacher_q)
-        grad_block = pl.pallas_call(
+        grad_block, dh, dw, loss = pl.pallas_call(
             table_kernel,
-            in_specs=[any_spec, any_spec],
-            out_specs=any_spec,
-            out_shape=jax.ShapeDtypeStruct((vocab, dim), F32),
+            in_specs=[any_spec, any_spec, any_spec, vmem_spec, vmem_spec],
+            out_specs=(any_spec, any_spec, vmem_spec, vmem_spec),
+            out_shape=(
+                jax.ShapeDtypeStruct((vocab, dim), F32),
+                jax.ShapeDtypeStruct((tokens, dim), BF16),
+                jax.ShapeDtypeStruct((dim,), F32),
+                jax.ShapeDtypeStruct((1, 128), F32),
+            ),
             scratch_shapes=[
                 vm((tokens, vocab), BF16),
                 vm((tokens, dim), BF16),
-                vm((SLOTS, VT, dim), F32),
+                vm((SLOTS, TT, dim), F32),
+                vm((tokens, dim), BF16),
                 dma,
-                dma((vocab // VT,)),
-                dma((SLOTS,)),
+                dma((vocab // TT,)),
+                dma((SLOTS, 2)),
+                dma((2,)),
             ],
             compiler_params=pltpu.CompilerParams(vmem_limit_bytes=67_043_328),
             name='table_grad',
-        )(dz, x_in)
+        )(dz, x_in, dh, dw, loss)
         return (loss[0, 0:1], dh, dw, grad_block)
 
     return jax.shard_map(local_step, mesh=mesh, in_specs=(P('dp', None), P(None), P('tp', None), P('dp', None), P('dp', None)), out_specs=(P('dp'), P('dp', None), P('dp'), P(('dp', 'tp'), None)), check_vma=False)

time: 118 us -> 109 us (0.924)
  local copies, waits for them, and re-layouts: 4.01 us -> 0 us
  Pallas kernels: 111 us -> 108 us
  between operations: 2.46 us -> 0.64 us
    pallas_call x1, Pallas kernels: 93.2 us -> 89 us  [local_step(): pl.pallas_call(lambda *refs: fused_kernel(n_dev, *refs), out_shape=(jax.S...]
    unnamed x4 -> x0, local copies, waits for them, and re-layouts: 4.01 us -> none
where the time goes in v3:
time: 109 us; the launch traced here: 108 us
  Pallas kernels  108 us (99%)
    pallas_call x1, Pallas kernels, local_step(): pl.pallas_call(lambda *refs: fused_kernel(n_dev, *refs), out_shape=(jax.S...  89 us
    pallas_call x1, Pallas kernels, local_step(): pl.pallas_call(table_kernel, in_specs=[any_spec, any_spec, any_spec, vmem...  18.6 us

profile of v3, /device:TPU:1, one launch (start us, length us, event | category | flops | bytes accessed | tf_op | source)
XLA Modules:
  0.0 108.2 jit_solution(12207894831201923137)
XLA Ops:
  0.6 89.0 %fused_head.1 = (bf16[512,2560]{1,0:T(8,128)(2,1)}, f32[2560]{0:T(1024)}, f32[1,128]{1,0:T(1,128)}, bf16[512,4096]{1,0:T(8,128)(2,1)}, bf16[512,2560]{1,0:T(8,128)(2,1)}) custom-call(bf16[512,2560]{1,0:T(8,128)(2,1)} %refs_0_.1, f32[2560]{0:T(1024)} %refs_1_.1, bf16[4096,2560]{1,0:T(8,128)(2,1)} %refs_2_.1, s32[512,256]{1,0:T(8,128)} %refs_3_.1, ...), custom_call_target="tpu_custom_call" | custom-call | tf_op jit(solution)/shard_map/fused_head/pallas_call | solution.py:445
  89.6 18.6 %table_grad.1 = (f32[4096,2560]{1,0:T(8,128)}, bf16[512,2560]{1,0:T(8,128)(2,1)}, f32[2560]{0:T(1024)}, f32[1,128]{1,0:T(1,128)}) custom-call(bf16[512,4096]{1,0:T(8,128)(2,1)} %get-tuple-element.13.dz_hbm, bf16[512,2560]{1,0:T(8,128)(2,1)} %get-tuple-element.14.x_hbm, bf16[512,2560]{1,0:T(8,128)(2,1)} %get-tuple-element.15.dh_hbm, ...), custom_call_target="tpu_custom_call" | custom-call | tf_op jit(solution)/shard_map/table_grad/pallas_call | solution.py:495

commit v4 on v3

--- a/solution.py
+++ b/solution.py
@@ -11,6 +11,7 @@
 NT = (((1,), (1,)), ((), ()))
 TN = (((0,), (0,)), ((), ()))
 CHUNKS = 4
+HALVES = 2
 VT = 256
 SLOTS = 3
 TT = 512
@@ -72,50 +73,43 @@
     h_copy.wait()
     gain = w_ref[...].reshape(1, dim) + 1.0
 
-    @pl.loop(0, tokens // 64)
-    def _(i):
-        rows = pl.ds(al(i * 64, 64), 64)
-        acc = jnp.zeros((64, 128), F32)
-        for k in range(dim // 128):
-            hf = h_v[rows, 128 * k:128 * (k + 1)].astype(F32)
-            acc = acc + hf * hf
-        inv = lax.rsqrt(jnp.sum(acc, axis=1, keepdims=True) * (1.0 / dim) + 1e-6)
-        inv = jnp.broadcast_to(inv, (64, 128))
-        for k in range(dim // 128):
-            hf = h_v[rows, 128 * k:128 * (k + 1)].astype(F32)
-            x_v[rows, 128 * k:128 * (k + 1)] = (hf * inv * gain[:, 128 * k:128 * (k + 1)]).astype(BF16)
-
-    x_copy = pltpu.make_async_copy(x_v, x_hbm, out_sem.at[0])
-    x_copy.start()
+    part = tokens // HALVES
+
+    def norm(h):
+        @pl.loop(0, part // 64)
+        def _(i):
+            rows = pl.ds(al(h * part + i * 64, 64), 64)
+            acc = jnp.zeros((64, 128), F32)
+            for k in range(dim // 128):
+                hf = h_v[rows, 128 * k:128 * (k + 1)].astype(F32)
+                acc = acc + hf * hf
+            inv = lax.rsqrt(jnp.sum(acc, axis=1, keepdims=True) * (1.0 / dim) + 1e-6)
+            inv = jnp.broadcast_to(inv, (64, 128))
+            for k in range(dim // 128):
+                hf = h_v[rows, 128 * k:128 * (k + 1)].astype(F32)
+                x_v[rows, 128 * k:128 * (k + 1)] = (hf * inv * gain[:, 128 * k:128 * (k + 1)]).astype(BF16)
 
     mx_v[...] = jnp.full(mx_v.shape, -jnp.inf, F32)
     sm_v[...] = jnp.zeros(sm_v.shape, F32)
 
-    @pl.loop(0, n_blk)
-    def _(i):
-        e_copy(i).wait()
-        zb = lax.dot_general(x_v[...], e_v[pl.ds(al(i * VT, VT), VT), :], NT, preferred_element_type=F32)
-        z_v[:, pl.ds(al(i * VT, VT), VT)] = zb
-        old = mx_v[...]
-        new = old
-        for k in range(VT // 128):
-            new = jnp.maximum(new, zb[:, 128 * k:128 * (k + 1)])
-        total = sm_v[...] * jnp.exp(old - new)
-        for k in range(VT // 128):
-            total = total + jnp.exp(zb[:, 128 * k:128 * (k + 1)] - new)
-        mx_v[...] = new
-        sm_v[...] = total
-
-    for b in range(tokens // 128):
-        span = slice(128 * b, 128 * (b + 1))
-        peaks = mx_v[span, :].T
-        peak = jnp.max(peaks, axis=0, keepdims=True)
-        st_send[:, 128 * b:128 * (b + 1)] = peak
-        st_send[:, tokens + 128 * b:tokens + 128 * (b + 1)] = jnp.sum(
-            sm_v[span, :].T * jnp.exp(peaks - peak), axis=0, keepdims=True)
-    st_recv[me] = st_send[...]
-
-    pl.semaphore_wait(barrier, n_dev - 1)
+    def logits(h, first, last):
+        rows = slice(h * part, (h + 1) * part)
+
+        @pl.loop(first, last)
+        def _(i):
+            if h == 0:
+                e_copy(i).wait()
+            zb = lax.dot_general(x_v[rows, :], e_v[pl.ds(al(i * VT, VT), VT), :], NT, preferred_element_type=F32)
+            z_v[rows, pl.ds(al(i * VT, VT), VT)] = zb
+            old = mx_v[rows, :]
+            new = old
+            for k in range(VT // 128):
+                new = jnp.maximum(new, zb[:, 128 * k:128 * (k + 1)])
+            total = sm_v[rows, :] * jnp.exp(old - new)
+            for k in range(VT // 128):
+                total = total + jnp.exp(zb[:, 128 * k:128 * (k + 1)] - new)
+            mx_v[rows, :] = new
+            sm_v[rows, :] = total
 
     def gather_copies(src, dst, s_sem, r_sem):
         out = []
@@ -125,17 +119,49 @@
                 device_id=(dp, (me + i) % n_dev), device_id_type=MESH))
         return out
 
-    st_copies = gather_copies(st_send, st_recv, st_ss, st_rs)
-    for copy in st_copies:
-        copy.start()
-
+    st_copies = [gather_copies(st_send.at[h], st_recv.at[h], st_ss.at[h], st_rs.at[h]) for h in range(HALVES)]
+
+    def send_stats(h):
+        for b in range(part // 128):
+            span = slice(h * part + 128 * b, h * part + 128 * (b + 1))
+            peaks = mx_v[span, :].T
+            peak = jnp.max(peaks, axis=0, keepdims=True)
+            st_send[h, :, 128 * b:128 * (b + 1)] = peak
+            st_send[h, :, part + 128 * b:part + 128 * (b + 1)] = jnp.sum(
+                sm_v[span, :].T * jnp.exp(peaks - peak), axis=0, keepdims=True)
+        st_recv[h, me] = st_send[h]
+        if h == 0:
+            pl.semaphore_wait(barrier, n_dev - 1)
+        for copy in st_copies[h]:
+            copy.start()
+
+    def take_stats(h):
+        for copy in st_copies[h]:
+            copy.wait_recv()
+        peak = st_recv[h, 0][:, 0:part]
+        for d in range(1, n_dev):
+            peak = jnp.maximum(peak, st_recv[h, d][:, 0:part])
+        total = jnp.zeros((1, part), F32)
+        for d in range(n_dev):
+            total = total + st_recv[h, d][:, part:2 * part] * jnp.exp(st_recv[h, d][:, 0:part] - peak)
+        log_z = peak + jnp.log(total)
+        for b in range(part // 128):
+            lz_v[h * part + 128 * b:h * part + 128 * (b + 1), :] = jnp.broadcast_to(
+                log_z[:, 128 * b:128 * (b + 1)], (128, 128)).T
+
+    norm(0)
+    logits(0, 0, n_blk)
+    send_stats(0)
+    norm(1)
+    x_copy = pltpu.make_async_copy(x_v, x_hbm, out_sem.at[0])
+    x_copy.start()
     ids_copy.wait()
 
     iota_hi = lax.broadcasted_iota(jnp.int32, (groups, 256), 0)
     iota_lo = lax.broadcasted_iota(jnp.int32, (128, 256), 0)
 
-    def build_q(c):
-        @pl.loop(0, rows_c // TOK)
+    def build_q(c, p):
+        @pl.loop(p * rows_c // TOK // 2, (p + 1) * rows_c // TOK // 2)
         def _(t):
             for u in range(TOK):
                 local = t * TOK + u
@@ -169,10 +195,10 @@
                 dz_v[rows, 128 * k:128 * (k + 1)] = d.astype(BF16)
             qz_v[...] = qz_v[...] + acc
 
-    def make_dx(c):
+    def make_dx(c, p):
         rows = slice(c * rows_c, (c + 1) * rows_c)
 
-        @pl.loop(0, dim // 256)
+        @pl.loop(p * dim // 256 // 2, (p + 1) * dim // 256 // 2)
         def _(j):
             cols = pl.ds(al(j * 256, 256), 256)
             dx_v[rows, cols] = jnp.dot(dz_v[rows, :], e_v[:, cols], preferred_element_type=F32)
@@ -181,9 +207,12 @@
     q4 = half // 4
     q2 = half // 2
 
-    def rcopy(src, dst, c, slot, dev):
+    wide = dim // 2
+    cut = (slice(0, wide), slice(wide, 2 * wide))
+
+    def rcopy(src, dst, c, p, slot, dev):
         return pltpu.make_async_remote_copy(
-            src_ref=src, dst_ref=dst, send_sem=ss.at[c, slot], recv_sem=rs.at[c, slot],
+            src_ref=src, dst_ref=dst, send_sem=ss.at[c, p, slot], recv_sem=rs.at[c, p, slot],
             device_id=(dp, dev), device_id_type=MESH)
 
     def mine(c):
@@ -196,53 +225,58 @@
             copy.start()
             sent.append(copy)
 
-    def s0(c):
-        return rcopy(dx_v.at[pl.ds(al(c * rows_c + half * (1 - core), half), half)], r0_v.at[c], c, 0, sib)
-
-    def s1(c):
-        a = rcopy(dx_v.at[pl.ds(al(mine(c) + q4 * (1 - xc), q4), q4)], r1_v.at[c, 0], c, 1, xn)
-        b = rcopy(dx_v.at[pl.ds(al(mine(c) + q2 + q4 * (1 - yc), q4), q4)], r1_v.at[c, 1], c, 2, yn)
+    def dx_at(start, size, p):
+        return dx_v.at[pl.ds(al(start, size), size), cut[p]]
+
+    def g_at(start, size, p):
+        return g_v.at[pl.ds(al(start, size), size), cut[p]]
+
+    def s0(c, p):
+        return rcopy(dx_at(c * rows_c + half * (1 - core), half, p), r0_v.at[c, :, cut[p]], c, p, 0, sib)
+
+    def s1(c, p):
+        a = rcopy(dx_at(mine(c) + q4 * (1 - xc), q4, p), r1_v.at[c, 0, :, cut[p]], c, p, 1, xn)
+        b = rcopy(dx_at(mine(c) + q2 + q4 * (1 - yc), q4, p), r1_v.at[c, 1, :, cut[p]], c, p, 2, yn)
         return a, b
 
-    def s2(c):
-        a = rcopy(dx_v.at[pl.ds(al(mine(c) + q4 * xc + q8 * (1 - yc), q8), q8)], r2_v.at[c, 0], c, 3, yn)
-        b = rcopy(dx_v.at[pl.ds(al(mine(c) + q2 + q4 * yc + q8 * (1 - xc), q8), q8)], r2_v.at[c, 1], c, 4, xn)
+    def s2(c, p):
+        a = rcopy(dx_at(mine(c) + q4 * xc + q8 * (1 - yc), q8, p), r2_v.at[c, 0, :, cut[p]], c, p, 3, yn)
+        b = rcopy(dx_at(mine(c) + q2 + q4 * yc + q8 * (1 - xc), q8, p), r2_v.at[c, 1, :, cut[p]], c, p, 4, xn)
         return a, b
 
-    def s3(c):
-        rows_a = pl.ds(al(mine(c) + q4 * xc + q8 * yc, q8), q8)
-        rows_b = pl.ds(al(mine(c) + q2 + q4 * yc + q8 * xc, q8), q8)
-        return (rcopy(g_v.at[rows_a], g_v.at[rows_a], c, 5, yn), rcopy(g_v.at[rows_b], g_v.at[rows_b], c, 6, xn))
-
-    def s4(c):
-        rows_a = pl.ds(al(mine(c) + q4 * xc, q4), q4)
-        rows_b = pl.ds(al(mine(c) + q2 + q4 * yc, q4), q4)
-        return (rcopy(g_v.at[rows_a], g_v.at[rows_a], c, 7, xn), rcopy(g_v.at[rows_b], g_v.at[rows_b], c, 8, yn))
-
-    def s5(c):
-        rows = pl.ds(al(mine(c), half), half)
-        return rcopy(g_v.at[rows], g_v.at[rows], c, 9, sib)
-
-    def f0(c):
-        go(s0(c))
-
-    def f1(c):
-        s0(c).wait_recv()
+    def s3(c, p):
+        a = g_at(mine(c) + q4 * xc + q8 * yc, q8, p)
+        b = g_at(mine(c) + q2 + q4 * yc + q8 * xc, q8, p)
+        return rcopy(a, a, c, p, 5, yn), rcopy(b, b, c, p, 6, xn)
+
+    def s4(c, p):
+        a = g_at(mine(c) + q4 * xc, q4, p)
+        b = g_at(mine(c) + q2 + q4 * yc, q4, p)
+        return rcopy(a, a, c, p, 7, xn), rcopy(b, b, c, p, 8, yn)
+
+    def s5(c, p):
+        a = g_at(mine(c), half, p)
+        return rcopy(a, a, c, p, 9, sib)
+
+    def f0(c, p):
+        go(s0(c, p))
+
+    def f1(c, p):
+        s0(c, p).wait_recv()
 
         @pl.loop(0, half // 8)
         def _(i):
             rows = pl.ds(al(mine(c) + 8 * i, 8), 8)
-            dx_v[rows, :] = dx_v[rows, :] + r0_v[c, pl.ds(al(8 * i, 8), 8), :]
-        go(*s1(c))
-
-    def f2(c):
-        a, b = s1(c)
-        a.wait_recv()
-        b.wait_recv()
+            dx_v[rows, cut[p]] = dx_v[rows, cut[p]] + r0_v[c, pl.ds(al(8 * i, 8), 8), cut[p]]
+        go(*s1(c, p))
+
+    def f2(c, p):
+        for copy in s1(c, p):
+            copy.wait_recv()
         for k, start in ((0, mine(c) + q4 * xc), (1, mine(c) + q2 + q4 * yc)):
             rows = pl.ds(al(start, q4), q4)
-            dx_v[rows, :] = dx_v[rows, :] + r1_v[c, k]
-        go(*s2(c))
+            dx_v[rows, cut[p]] = dx_v[rows, cut[p]] + r1_v[c, k, :, cut[p]]
+        go(*s2(c, p))
 
     def norm_back(c, k, block, side):
         rows16 = pl.ds(al(block, 16), 16)
@@ -257,24 +291,23 @@
         dwacc_v[...] = dwacc_v[...] + grad * hf * inv
 
     def f3(c):
-        a, b = s2(c)
-        a.wait_recv()
-        b.wait_recv()
+        for p in range(2):
+            for copy in s2(c, p):
+                copy.wait_recv()
         norm_back(c, 0, mine(c) + q4 * xc, yc)
         norm_back(c, 1, mine(c) + q2 + q4 * yc, xc)
-        go(*s3(c))
-
-    def f4(c):
-        a, b = s3(c)
-        a.wait_recv()
-        b.wait_recv()
-        go(*s4(c))
-
-    def f5(c):
-        a, b = s4(c)
-        a.wait_recv()
-        b.wait_recv()
-        go(s5(c))
+        for p in range(2):
+            go(*s3(c, p))
+
+    def f4(c, p):
+        for copy in s3(c, p):
+            copy.wait_recv()
+        go(*s4(c, p))
+
+    def f5(c, p):
+        for copy in s4(c, p):
+            copy.wait_recv()
+        go(s5(c, p))
 
     def rows_of(c):
         return slice(c * rows_c, (c + 1) * rows_c)
@@ -286,7 +319,8 @@
         return pltpu.make_async_copy(dz_v.at[rows_of(c)], dz_hbm.at[rows_of(c)], out_sem.at[1 + CHUNKS + c])
 
     def f6(c):
-        s5(c).wait_recv()
+        for p in range(2):
+            s5(c, p).wait_recv()
 
         @pl.loop(0, rows_c // 16)
         def _(i):
@@ -296,54 +330,80 @@
 
     dwacc_v[...] = jnp.zeros(dwacc_v.shape, F32)
     qz_v[...] = jnp.zeros(qz_v.shape, F32)
-    build_q(0)
-
-    for copy in st_copies:
-        copy.wait_recv()
-    peak = st_recv[0][:, 0:tokens]
-    for d in range(1, n_dev):
-        peak = jnp.maximum(peak, st_recv[d][:, 0:tokens])
-    total = jnp.zeros((1, tokens), F32)
-    for d in range(n_dev):
-        total = total + st_recv[d][:, tokens:2 * tokens] * jnp.exp(st_recv[d][:, 0:tokens] - peak)
-    log_z = peak + jnp.log(total)
-    for b in range(tokens // 128):
-        lz_v[128 * b:128 * (b + 1), :] = jnp.broadcast_to(log_z[:, 128 * b:128 * (b + 1)], (128, 128)).T
-
-    def chunk(c):
+
+    def finish_dz(c):
         make_dz(c)
         dz_copy(c).start()
-        make_dx(c)
-
-    chunk(0)
-    f0(0)
-    build_q(1)
-    f1(0)
-    chunk(1)
-    f0(1)
-    f2(0)
-    build_q(2)
-    f1(1)
+
+    quarter = n_blk // 4
+    build_q(0, 0)
+    build_q(0, 1)
+    take_stats(0)
+    finish_dz(0)
+    make_dx(0, 0)
+    f0(0, 0)
+    make_dx(0, 1)
+    f0(0, 1)
+    f1(0, 0)
+    build_q(1, 0)
+    f1(0, 1)
+    build_q(1, 1)
+    f2(0, 0)
+    finish_dz(1)
+    f2(0, 1)
+    make_dx(1, 0)
+    f0(1, 0)
+    make_dx(1, 1)
+    f0(1, 1)
     f3(0)
-    chunk(2)
-    f0(2)
-    f2(1)
-    f4(0)
-    build_q(3)
-    f1(2)
+    f1(1, 0)
+    logits(1, 0, quarter)
+    f1(1, 1)
+    f4(0, 0)
+    f4(0, 1)
+    logits(1, quarter, 2 * quarter)
+    f2(1, 0)
+    logits(1, 2 * quarter, 3 * quarter)
+    f2(1, 1)
+    f5(0, 0)
+    f5(0, 1)
+    logits(1, 3 * quarter, n_blk)
+    send_stats(1)
     f3(1)
-    f5(0)
-    chunk(3)
-    f0(3)
-    f2(2)
-    f4(1)
     f6(0)
-    f1(3)
+    build_q(2, 0)
+    build_q(2, 1)
+    f4(1, 0)
+    f4(1, 1)
+    take_stats(1)
+    finish_dz(2)
+    make_dx(2, 0)
+    f0(2, 0)
+    f5(1, 0)
+    f5(1, 1)
+    make_dx(2, 1)
+    f0(2, 1)
+    f1(2, 0)
+    build_q(3, 0)
+    f1(2, 1)
+    build_q(3, 1)
+    f2(2, 0)
+    f6(1)
+    finish_dz(3)
+    f2(2, 1)
+    make_dx(3, 0)
+    f0(3, 0)
+    make_dx(3, 1)
+    f0(3, 1)
+    f1(3, 0)
     f3(2)
-    f5(1)
-    f2(3)
-    f4(2)
-    f6(1)
+    f1(3, 1)
+    f2(3, 0)
+    f4(2, 0)
+    f4(2, 1)
+    f2(3, 1)
+    f5(2, 0)
+    f5(2, 1)
     f3(3)
     fin_send[:, 0:dim] = jnp.sum(dwacc_v[...], axis=0, keepdims=True)
     fin_send[:, dim:dim + 128] = jnp.sum(qz_v[...], axis=0, keepdims=True)
@@ -351,10 +411,11 @@
     fin_copies = gather_copies(fin_send, fin_recv, fin_ss, fin_rs)
     for copy in fin_copies:
         copy.start()
-    f5(2)
-    f4(3)
+    f4(3, 0)
+    f4(3, 1)
     f6(2)
-    f5(3)
+    f5(3, 0)
+    f5(3, 1)
 
     for copy in fin_copies:
         copy.wait_recv()
@@ -366,7 +427,7 @@
     loss_ref[...] = (weighted - jnp.sum(fin[:, dim:dim + 128])) * inv_tokens
     f6(3)
 
-    for copy in st_copies + sent + fin_copies:
+    for copy in st_copies[0] + st_copies[1] + sent + fin_copies:
         copy.wait_send()
     x_copy.wait()
     for c in range(CHUNKS):
@@ -472,8 +533,8 @@
                 vm((CHUNKS, half, dim), F32),
                 vm((CHUNKS, 2, half // 4, dim), F32),
                 vm((CHUNKS, 2, half // 8, dim), F32),
-                vm((1, 2 * tokens), F32),
-                vm((n_dev, 1, 2 * tokens), F32),
+                vm((HALVES, 1, 2 * tokens // HALVES), F32),
+                vm((HALVES, n_dev, 1, 2 * tokens // HALVES), F32),
                 vm((1, dim + 128), F32),
                 vm((n_dev, 1, dim + 128), F32),
                 vm((8, dim), F32),
@@ -481,12 +542,12 @@
                 dma((vocab // VT,)),
                 dma((3,)),
                 dma((1 + 2 * CHUNKS,)),
+                dma((HALVES, n_dev - 1)),
+                dma((HALVES, n_dev - 1)),
                 dma((n_dev - 1,)),
                 dma((n_dev - 1,)),
-                dma((n_dev - 1,)),
-                dma((n_dev - 1,)),
-                dma((CHUNKS, 10)),
-                dma((CHUNKS, 10)),
+                dma((CHUNKS, 2, 10)),
+                dma((CHUNKS, 2, 10)),
             ],
             compiler_params=pltpu.CompilerParams(
                 collective_id=0, has_side_effects=True, vmem_limit_bytes=67_043_328),

time: 109 us -> 113 us (1.037)
  Pallas kernels: 108 us -> 112 us
    pallas_call x1, Pallas kernels: 89 us -> 93.8 us  [local_step(): pl.pallas_call(lambda *refs: fused_kernel(n_dev, *refs), out_shape=(jax.S...]
where the time goes in v4:
time: 113 us
  Pallas kernels  112 us (99%)
    pallas_call x1, Pallas kernels, local_step(): pl.pallas_call(lambda *refs: fused_kernel(n_dev, *refs), out_shape=(jax.S...  93.8 us
    pallas_call x1, Pallas kernels, local_step(): pl.pallas_call(table_kernel, in_specs=[any_spec, any_spec, any_spec, vmem...  18.6 us

profile of v4, /device:TPU:1, one launch (start us, length us, event | category | flops | bytes accessed | tf_op | source)
XLA Modules:
  0.0 113.0 jit_solution(4086411670312724228)
XLA Ops:
  0.6 93.8 %fused_head.1 = (bf16[512,2560]{1,0:T(8,128)(2,1)}, f32[2560]{0:T(1024)}, f32[1,128]{1,0:T(1,128)}, bf16[512,4096]{1,0:T(8,128)(2,1)}, bf16[512,2560]{1,0:T(8,128)(2,1)}) custom-call(bf16[512,2560]{1,0:T(8,128)(2,1)} %refs_0_.1, f32[2560]{0:T(1024)} %refs_1_.1, bf16[4096,2560]{1,0:T(8,128)(2,1)} %refs_2_.1, s32[512,256]{1,0:T(8,128)} %refs_3_.1, ...), custom_call_target="tpu_custom_call" | custom-call | tf_op jit(solution)/shard_map/fused_head/pallas_call | solution.py:506
  94.5 18.6 %table_grad.1 = (f32[4096,2560]{1,0:T(8,128)}, bf16[512,2560]{1,0:T(8,128)(2,1)}, f32[2560]{0:T(1024)}, f32[1,128]{1,0:T(1,128)}) custom-call(bf16[512,4096]{1,0:T(8,128)(2,1)} %get-tuple-element.13.dz_hbm, bf16[512,2560]{1,0:T(8,128)(2,1)} %get-tuple-element.14.x_hbm, bf16[512,2560]{1,0:T(8,128)(2,1)} %get-tuple-element.15.dh_hbm, ...), custom_call_target="tpu_custom_call" | custom-call | tf_op jit(solution)/shard_map/table_grad/pallas_call | solution.py:556

commit v5 on v4

--- a/solution.py
+++ b/solution.py
@@ -12,7 +12,7 @@
 TN = (((0,), (0,)), ((), ()))
 CHUNKS = 4
 HALVES = 2
-VT = 256
+VT = 512
 SLOTS = 3
 TT = 512
 TOK = 32
@@ -344,66 +344,63 @@
     f0(0, 0)
     make_dx(0, 1)
     f0(0, 1)
+    build_q(1, 0)
     f1(0, 0)
-    build_q(1, 0)
+    build_q(1, 1)
     f1(0, 1)
-    build_q(1, 1)
-    f2(0, 0)
     finish_dz(1)
-    f2(0, 1)
     make_dx(1, 0)
     f0(1, 0)
     make_dx(1, 1)
     f0(1, 1)
+    f2(0, 0)
+    logits(1, 0, quarter)
+    f1(1, 0)
+    f2(0, 1)
+    logits(1, quarter, 2 * quarter)
+    f1(1, 1)
+    logits(1, 2 * quarter, n_blk)
+    send_stats(1)
     f3(0)
-    f1(1, 0)
-    logits(1, 0, quarter)
-    f1(1, 1)
-    f4(0, 0)
-    f4(0, 1)
-    logits(1, quarter, 2 * quarter)
     f2(1, 0)
-    logits(1, 2 * quarter, 3 * quarter)
+    build_q(2, 0)
     f2(1, 1)
-    f5(0, 0)
-    f5(0, 1)
-    logits(1, 3 * quarter, n_blk)
-    send_stats(1)
-    f3(1)
-    f6(0)
-    build_q(2, 0)
     build_q(2, 1)
-    f4(1, 0)
-    f4(1, 1)
     take_stats(1)
     finish_dz(2)
     make_dx(2, 0)
     f0(2, 0)
-    f5(1, 0)
-    f5(1, 1)
+    f4(0, 0)
+    f4(0, 1)
+    f3(1)
     make_dx(2, 1)
     f0(2, 1)
+    build_q(3, 0)
     f1(2, 0)
-    build_q(3, 0)
+    build_q(3, 1)
     f1(2, 1)
-    build_q(3, 1)
-    f2(2, 0)
-    f6(1)
+    f4(1, 0)
+    f4(1, 1)
     finish_dz(3)
-    f2(2, 1)
     make_dx(3, 0)
     f0(3, 0)
+    f5(0, 0)
+    f5(0, 1)
     make_dx(3, 1)
     f0(3, 1)
     f1(3, 0)
+    f2(2, 0)
+    f2(2, 1)
+    f5(1, 0)
+    f5(1, 1)
+    f1(3, 1)
+    f6(0)
+    f2(3, 0)
     f3(2)
-    f1(3, 1)
-    f2(3, 0)
+    f2(3, 1)
+    f6(1)
     f4(2, 0)
     f4(2, 1)
-    f2(3, 1)
-    f5(2, 0)
-    f5(2, 1)
     f3(3)
     fin_send[:, 0:dim] = jnp.sum(dwacc_v[...], axis=0, keepdims=True)
     fin_send[:, dim:dim + 128] = jnp.sum(qz_v[...], axis=0, keepdims=True)
@@ -411,6 +408,8 @@
     fin_copies = gather_copies(fin_send, fin_recv, fin_ss, fin_rs)
     for copy in fin_copies:
         copy.start()
+    f5(2, 0)
+    f5(2, 1)
     f4(3, 0)
     f4(3, 1)
     f6(2)

time: 113 us -> 105 us (0.929)
  Pallas kernels: 112 us -> 104 us
    pallas_call x1, Pallas kernels: 93.8 us -> 85.8 us  [local_step(): pl.pallas_call(lambda *refs: fused_kernel(n_dev, *refs), out_shape=(jax.S...]
where the time goes in v5:
time: 105 us
  Pallas kernels  104 us (99%)
    pallas_call x1, Pallas kernels, local_step(): pl.pallas_call(lambda *refs: fused_kernel(n_dev, *refs), out_shape=(jax.S...  85.8 us
    pallas_call x1, Pallas kernels, local_step(): pl.pallas_call(table_kernel, in_specs=[any_spec, any_spec, any_spec, vmem...  18.6 us

profile of v5, /device:TPU:1, one launch (start us, length us, event | category | flops | bytes accessed | tf_op | source)
XLA Modules:
  0.0 105.1 jit_solution(2557580682460791136)
XLA Ops:
  0.6 85.8 %fused_head.1 = (bf16[512,2560]{1,0:T(8,128)(2,1)}, f32[2560]{0:T(1024)}, f32[1,128]{1,0:T(1,128)}, bf16[512,4096]{1,0:T(8,128)(2,1)}, bf16[512,2560]{1,0:T(8,128)(2,1)}) custom-call(bf16[512,2560]{1,0:T(8,128)(2,1)} %refs_0_.1, f32[2560]{0:T(1024)} %refs_1_.1, bf16[4096,2560]{1,0:T(8,128)(2,1)} %refs_2_.1, s32[512,256]{1,0:T(8,128)} %refs_3_.1, ...), custom_call_target="tpu_custom_call" | custom-call | tf_op jit(solution)/shard_map/fused_head/pallas_call | solution.py:505
  86.4 18.6 %table_grad.1 = (f32[4096,2560]{1,0:T(8,128)}, bf16[512,2560]{1,0:T(8,128)(2,1)}, f32[2560]{0:T(1024)}, f32[1,128]{1,0:T(1,128)}) custom-call(bf16[512,4096]{1,0:T(8,128)(2,1)} %get-tuple-element.13.dz_hbm, bf16[512,2560]{1,0:T(8,128)(2,1)} %get-tuple-element.14.x_hbm, bf16[512,2560]{1,0:T(8,128)(2,1)} %get-tuple-element.15.dh_hbm, ...), custom_call_target="tpu_custom_call" | custom-call | tf_op jit(solution)/shard_map/table_grad/pallas_call | solution.py:555

commit v6 on v5

--- a/solution.py
+++ b/solution.py
@@ -43,11 +43,16 @@
     def al(value, mult):
         return pl.multiple_of(value, mult)
 
-    h_copy = pltpu.make_async_copy(h_hbm, h_v, in_sem.at[0])
+    part = tokens // HALVES
+
+    def h_copy(h):
+        rows = slice(h * part, (h + 1) * part)
+        return pltpu.make_async_copy(h_hbm.at[rows], h_v.at[rows], in_sem.at[3 * h])
+
     ids_copy = pltpu.make_async_copy(ids_hbm, ids_v, in_sem.at[1])
     q_copy = pltpu.make_async_copy(q_hbm, q_v, in_sem.at[2])
     q_copy.start()
-    h_copy.start()
+    h_copy(0).start()
 
     def e_copy(i):
         rows = pl.ds(al(i * VT, VT), VT)
@@ -57,6 +62,7 @@
     def _(i):
         e_copy(i).start()
 
+    h_copy(1).start()
     ids_copy.start()
 
     barrier = pltpu.get_barrier_semaphore()
@@ -70,12 +76,11 @@
         rows = pl.ds(al(i * 64, 64), 64)
         sn_v[rows, :] = jnp.broadcast_to(jnp.sum(q_v[rows, :], axis=1, keepdims=True), (64, 128))
 
-    h_copy.wait()
     gain = w_ref[...].reshape(1, dim) + 1.0
 
-    part = tokens // HALVES
-
     def norm(h):
+        h_copy(h).wait()
+
         @pl.loop(0, part // 64)
         def _(i):
             rows = pl.ds(al(h * part + i * 64, 64), 64)
@@ -148,14 +153,6 @@
         for b in range(part // 128):
             lz_v[h * part + 128 * b:h * part + 128 * (b + 1), :] = jnp.broadcast_to(
                 log_z[:, 128 * b:128 * (b + 1)], (128, 128)).T
-
-    norm(0)
-    logits(0, 0, n_blk)
-    send_stats(0)
-    norm(1)
-    x_copy = pltpu.make_async_copy(x_v, x_hbm, out_sem.at[0])
-    x_copy.start()
-    ids_copy.wait()
 
     iota_hi = lax.broadcasted_iota(jnp.int32, (groups, 256), 0)
     iota_lo = lax.broadcasted_iota(jnp.int32, (128, 256), 0)
@@ -336,6 +333,13 @@
         dz_copy(c).start()
 
     quarter = n_blk // 4
+    norm(0)
+    logits(0, 0, n_blk)
+    send_stats(0)
+    norm(1)
+    x_copy = pltpu.make_async_copy(x_v, x_hbm, out_sem.at[0])
+    x_copy.start()
+    ids_copy.wait()
     build_q(0, 0)
     build_q(0, 1)
     take_stats(0)
@@ -349,72 +353,73 @@
     build_q(1, 1)
     f1(0, 1)
     finish_dz(1)
-    make_dx(1, 0)
-    f0(1, 0)
     make_dx(1, 1)
     f0(1, 1)
+    make_dx(1, 0)
     f2(0, 0)
+    f0(1, 0)
+    f2(0, 1)
     logits(1, 0, quarter)
+    f1(1, 1)
+    logits(1, quarter, 2 * quarter)
     f1(1, 0)
-    f2(0, 1)
-    logits(1, quarter, 2 * quarter)
-    f1(1, 1)
-    logits(1, 2 * quarter, n_blk)
+    logits(1, 2 * quarter, 3 * quarter)
+    f3(0)
+    logits(1, 3 * quarter, n_blk)
     send_stats(1)
-    f3(0)
+    f2(1, 1)
+    build_q(2, 0)
     f2(1, 0)
-    build_q(2, 0)
-    f2(1, 1)
+    f4(0, 0)
     build_q(2, 1)
+    f4(0, 1)
     take_stats(1)
     finish_dz(2)
     make_dx(2, 0)
     f0(2, 0)
-    f4(0, 0)
-    f4(0, 1)
     f3(1)
     make_dx(2, 1)
     f0(2, 1)
+    f1(2, 0)
     build_q(3, 0)
-    f1(2, 0)
+    f4(1, 0)
     build_q(3, 1)
+    finish_dz(3)
+    f4(1, 1)
     f1(2, 1)
-    f4(1, 0)
-    f4(1, 1)
-    finish_dz(3)
     make_dx(3, 0)
     f0(3, 0)
-    f5(0, 0)
     f5(0, 1)
+    f2(2, 0)
     make_dx(3, 1)
     f0(3, 1)
     f1(3, 0)
-    f2(2, 0)
     f2(2, 1)
-    f5(1, 0)
-    f5(1, 1)
     f1(3, 1)
-    f6(0)
     f2(3, 0)
     f3(2)
+    f5(0, 0)
     f2(3, 1)
-    f6(1)
     f4(2, 0)
+    f3(3)
+    f5(1, 0)
     f4(2, 1)
-    f3(3)
+    f5(2, 0)
     fin_send[:, 0:dim] = jnp.sum(dwacc_v[...], axis=0, keepdims=True)
     fin_send[:, dim:dim + 128] = jnp.sum(qz_v[...], axis=0, keepdims=True)
     fin_recv[me] = fin_send[...]
     fin_copies = gather_copies(fin_send, fin_recv, fin_ss, fin_rs)
     for copy in fin_copies:
         copy.start()
-    f5(2, 0)
-    f5(2, 1)
     f4(3, 0)
     f4(3, 1)
-    f6(2)
+    f6(0)
+    f5(1, 1)
+    f5(2, 1)
     f5(3, 0)
     f5(3, 1)
+    f6(2)
+    f6(1)
 
     for copy in fin_copies:
         copy.wait_recv()
@@ -449,10 +454,14 @@
         rows = pl.ds(pl.multiple_of(i * TT, TT), TT)
         return pltpu.make_async_copy(o_v.at[slot, :, cuts[k]], out_hbm.at[rows, cuts[k]], out_sem.at[slot, k])
 
-    x_copy = pltpu.make_async_copy(x_hbm, x_v, x_sem)
-    x_copy.start()
-
-    @pl.loop(0, n_blk)
+    def x_copy(k):
+        return pltpu.make_async_copy(x_hbm.at[:, cuts[k]], x_v.at[:, cuts[k]], x_sem.at[k])
+
+    dz_copy(0).start()
+    x_copy(0).start()
+    x_copy(1).start()
+
+    @pl.loop(1, n_blk)
     def _(i):
         dz_copy(i).start()
 
@@ -461,8 +470,8 @@
     dh_in.start()
     dw_out[...] = dw_ref[...]
     loss_out[...] = loss_ref[...]
-    x_copy.wait()
-
+    x_copy(0).wait()
+    x_copy(1).wait()
     @pl.loop(0, n_blk)
     def _(i):
         dz_copy(i).wait()
@@ -539,7 +548,7 @@
                 vm((8, dim), F32),
                 vm((16, 128), F32),
                 dma((vocab // VT,)),
-                dma((3,)),
+                dma((4,)),
                 dma((1 + 2 * CHUNKS,)),
                 dma((HALVES, n_dev - 1)),
                 dma((HALVES, n_dev - 1)),
@@ -567,7 +576,7 @@
                 vm((tokens, dim), BF16),
                 vm((SLOTS, TT, dim), F32),
                 vm((tokens, dim), BF16),
-                dma,
+                dma((2,)),
                 dma((vocab // TT,)),
                 dma((SLOTS, 2)),
                 dma((2,)),

time: 105 us -> 104 us (level)
    pallas_call x1, Pallas kernels: 85.8 us -> 84.1 us  [local_step(): pl.pallas_call(lambda *refs: fused_kernel(n_dev, *refs), out_shape=(jax.S...]
where the time goes in v6:
time: 104 us; the launch traced here: 103 us
  Pallas kernels  103 us (99%)
    pallas_call x1, Pallas kernels, local_step(): pl.pallas_call(lambda *refs: fused_kernel(n_dev, *refs), out_shape=(jax.S...  84.1 us
    pallas_call x1, Pallas kernels, local_step(): pl.pallas_call(table_kernel, in_specs=[any_spec, any_spec, any_spec, vmem...  18.6 us

profile of v6, /device:TPU:1, one launch (start us, length us, event | category | flops | bytes accessed | tf_op | source)
XLA Modules:
  0.0 103.5 jit_solution(5862175211357185682)
XLA Ops:
  0.6 84.1 %fused_head.1 = (bf16[512,2560]{1,0:T(8,128)(2,1)}, f32[2560]{0:T(1024)}, f32[1,128]{1,0:T(1,128)}, bf16[512,4096]{1,0:T(8,128)(2,1)}, bf16[512,2560]{1,0:T(8,128)(2,1)}) custom-call(bf16[512,2560]{1,0:T(8,128)(2,1)} %refs_0_.1, f32[2560]{0:T(1024)} %refs_1_.1, bf16[4096,2560]{1,0:T(8,128)(2,1)} %refs_2_.1, s32[512,256]{1,0:T(8,128)} %refs_3_.1, ...), custom_call_target="tpu_custom_call" | custom-call | tf_op jit(solution)/shard_map/fused_head/pallas_call | solution.py:514
  84.7 18.6 %table_grad.1 = (f32[4096,2560]{1,0:T(8,128)}, bf16[512,2560]{1,0:T(8,128)(2,1)}, f32[2560]{0:T(1024)}, f32[1,128]{1,0:T(1,128)}) custom-call(bf16[512,4096]{1,0:T(8,128)(2,1)} %get-tuple-element.13.dz_hbm, bf16[512,2560]{1,0:T(8,128)(2,1)} %get-tuple-element.14.x_hbm, bf16[512,2560]{1,0:T(8,128)(2,1)} %get-tuple-element.15.dh_hbm, ...), custom_call_target="tpu_custom_call" | custom-call | tf_op jit(solution)/shard_map/table_grad/pallas_call | solution.py:564

commit v7 on v6

--- a/solution.py
+++ b/solution.py
@@ -200,6 +200,14 @@
             cols = pl.ds(al(j * 256, 256), 256)
             dx_v[rows, cols] = jnp.dot(dz_v[rows, :], e_v[:, cols], preferred_element_type=F32)
 
+    def mdx2(c, p):
+        rows = slice(c * rows_c, (c + 2) * rows_c)
+
+        @pl.loop(p * dim // 256 // 2, (p + 1) * dim // 256 // 2)
+        def _(j):
+            cols = pl.ds(al(j * 256, 256), 256)
+            dx_v[rows, cols] = jnp.dot(dz_v[rows, :], e_v[:, cols], preferred_element_type=F32)
+
     q8 = half // 8
     q4 = half // 4
     q2 = half // 2
@@ -344,67 +352,65 @@
     build_q(0, 1)
     take_stats(0)
     finish_dz(0)
-    make_dx(0, 0)
+    build_q(1, 0)
+    build_q(1, 1)
+    finish_dz(1)
+    mdx2(0, 0)
     f0(0, 0)
-    make_dx(0, 1)
+    f0(1, 0)
+    mdx2(0, 1)
+    f0(1, 1)
+    f1(0, 0)
     f0(0, 1)
-    build_q(1, 0)
-    f1(0, 0)
-    build_q(1, 1)
+    logits(1, 0, quarter)
+    f1(1, 0)
+    logits(1, quarter, 2 * quarter)
+    f1(1, 1)
     f1(0, 1)
-    finish_dz(1)
-    make_dx(1, 1)
-    f0(1, 1)
-    make_dx(1, 0)
-    f2(0, 0)
-    f0(1, 0)
-    f2(0, 1)
-    logits(1, 0, quarter)
-    f1(1, 1)
-    logits(1, quarter, 2 * quarter)
-    f1(1, 0)
     logits(1, 2 * quarter, 3 * quarter)
-    f3(0)
+    f2(1, 0)
     logits(1, 3 * quarter, n_blk)
     send_stats(1)
     f2(1, 1)
+    f2(0, 0)
     build_q(2, 0)
-    f2(1, 0)
-    f4(0, 0)
+    f2(0, 1)
     build_q(2, 1)
-    f4(0, 1)
+    f3(1)
     take_stats(1)
     finish_dz(2)
-    make_dx(2, 0)
-    f0(2, 0)
-    f3(1)
+    f3(0)
     make_dx(2, 1)
     f0(2, 1)
-    f1(2, 0)
+    f4(1, 0)
+    f4(1, 1)
+    make_dx(2, 0)
+    f4(0, 1)
+    f0(2, 0)
     build_q(3, 0)
-    f4(1, 0)
+    f1(2, 1)
     build_q(3, 1)
     finish_dz(3)
-    f4(1, 1)
-    f1(2, 1)
+    f1(2, 0)
+    f4(0, 0)
+    make_dx(3, 1)
+    f2(2, 1)
+    f0(3, 1)
     make_dx(3, 0)
     f0(3, 0)
+    f2(2, 0)
+    f1(3, 1)
+    f1(3, 0)
     f5(0, 1)
-    f2(2, 0)
-    make_dx(3, 1)
-    f0(3, 1)
-    f1(3, 0)
-    f2(2, 1)
-    f1(3, 1)
+    f3(2)
+    f2(3, 1)
+    f5(0, 0)
+    f5(1, 1)
     f2(3, 0)
-    f3(2)
-    f5(0, 0)
-    f2(3, 1)
     f4(2, 0)
+    f5(1, 0)
     f3(3)
-    f5(1, 0)
     f4(2, 1)
-    f5(2, 0)
     fin_send[:, 0:dim] = jnp.sum(dwacc_v[...], axis=0, keepdims=True)
     fin_send[:, dim:dim + 128] = jnp.sum(qz_v[...], axis=0, keepdims=True)
     fin_recv[me] = fin_send[...]
@@ -414,12 +420,12 @@
     f4(3, 0)
     f4(3, 1)
     f6(0)
-    f5(1, 1)
+    f5(3, 0)
     f5(2, 1)
-    f5(3, 0)
+    f5(2, 0)
+    f6(1)
     f5(3, 1)
     f6(2)
-    f6(1)
 
     for copy in fin_copies:
         copy.wait_recv()

time: 104 us -> 102 us (0.981)
  Pallas kernels: 103 us -> 101 us
    pallas_call x1, Pallas kernels: 84.1 us -> 82.8 us  [local_step(): pl.pallas_call(lambda *refs: fused_kernel(n_dev, *refs), out_shape=(jax.S...]
where the time goes in v7:
time: 102 us
  Pallas kernels  101 us (99%)
    pallas_call x1, Pallas kernels, local_step(): pl.pallas_call(lambda *refs: fused_kernel(n_dev, *refs), out_shape=(jax.S...  82.8 us
    pallas_call x1, Pallas kernels, local_step(): pl.pallas_call(table_kernel, in_specs=[any_spec, any_spec, any_spec, vmem...  18.6 us

profile of v7, /device:TPU:1, one launch (start us, length us, event | category | flops | bytes accessed | tf_op | source)
XLA Modules:
  0.0 102.2 jit_solution(1866751014764506118)
XLA Ops:
  0.6 82.8 %fused_head.1 = (bf16[512,2560]{1,0:T(8,128)(2,1)}, f32[2560]{0:T(1024)}, f32[1,128]{1,0:T(1,128)}, bf16[512,4096]{1,0:T(8,128)(2,1)}, bf16[512,2560]{1,0:T(8,128)(2,1)}) custom-call(bf16[512,2560]{1,0:T(8,128)(2,1)} %refs_0_.1, f32[2560]{0:T(1024)} %refs_1_.1, bf16[4096,2560]{1,0:T(8,128)(2,1)} %refs_2_.1, s32[512,256]{1,0:T(8,128)} %refs_3_.1, ...), custom_call_target="tpu_custom_call" | custom-call | tf_op jit(solution)/shard_map/fused_head/pallas_call | solution.py:520
  83.4 18.6 %table_grad.1 = (f32[4096,2560]{1,0:T(8,128)}, bf16[512,2560]{1,0:T(8,128)(2,1)}, f32[2560]{0:T(1024)}, f32[1,128]{1,0:T(1,128)}) custom-call(bf16[512,4096]{1,0:T(8,128)(2,1)} %get-tuple-element.13.dz_hbm, bf16[512,2560]{1,0:T(8,128)(2,1)} %get-tuple-element.14.x_hbm, bf16[512,2560]{1,0:T(8,128)(2,1)} %get-tuple-element.15.dh_hbm, ...), custom_call_target="tpu_custom_call" | custom-call | tf_op jit(solution)/shard_map/table_grad/pallas_call | solution.py:570

commit v8 on v7

--- a/solution.py
+++ b/solution.py
@@ -332,6 +332,22 @@
             rows = pl.ds(al(c * rows_c + 16 * i, 16), 16)
             dh_v[rows, :] = g_v[rows, :].astype(BF16)
         dh_copy(c).start()
+
+    def last_copy(p):
+        rows = rows_of(CHUNKS - 1)
+        return pltpu.make_async_copy(
+            dh_v.at[rows, cut[p]], dh_hbm.at[rows, cut[p]], out_sem.at[CHUNKS if p == 0 else 1 + 2 * CHUNKS])
+
+    def f6_last():
+        c = CHUNKS - 1
+        for p in range(2):
+            s5(c, p).wait_recv()
+
+            @pl.loop(0, rows_c // 16)
+            def _(i):
+                rows = pl.ds(al(c * rows_c + 16 * i, 16), 16)
+                dh_v[rows, cut[p]] = g_v[rows, cut[p]].astype(BF16)
+            last_copy(p).start()
 
     dwacc_v[...] = jnp.zeros(dwacc_v.shape, F32)
     qz_v[...] = jnp.zeros(qz_v.shape, F32)
@@ -435,14 +451,17 @@
     dw_ref[...] = fin[:, 0:dim].reshape(dim)
     weighted = jnp.sum(lz_v[...] * sn_v[...], axis=0, keepdims=True)
     loss_ref[...] = (weighted - jnp.sum(fin[:, dim:dim + 128])) * inv_tokens
-    f6(3)
+    f6_last()
 
     for copy in st_copies[0] + st_copies[1] + sent + fin_copies:
         copy.wait_send()
     x_copy.wait()
     for c in range(CHUNKS):
         dz_copy(c).wait()
-        dh_copy(c).wait()
+        if c < CHUNKS - 1:
+            dh_copy(c).wait()
+    for p in range(2):
+        last_copy(p).wait()
 
 
 def table_kernel(dz_hbm, x_hbm, dh_hbm, dw_ref, loss_ref, out_hbm, dh_out, dw_out, loss_out,
@@ -555,7 +574,7 @@
                 vm((16, 128), F32),
                 dma((vocab // VT,)),
                 dma((4,)),
-                dma((1 + 2 * CHUNKS,)),
+                dma((2 + 2 * CHUNKS,)),
                 dma((HALVES, n_dev - 1)),
                 dma((HALVES, n_dev - 1)),
                 dma((n_dev - 1,)),

time: 102 us -> 102 us (level)
  no operation moved by 1% of the time
where the time goes in v8:
time: 102 us
  Pallas kernels  101 us (99%)
    pallas_call x1, Pallas kernels, local_step(): pl.pallas_call(lambda *refs: fused_kernel(n_dev, *refs), out_shape=(jax.S...  82.7 us
    pallas_call x1, Pallas kernels, local_step(): pl.pallas_call(table_kernel, in_specs=[any_spec, any_spec, any_spec, vmem...  18.6 us

profile of v8, /device:TPU:1, one launch (start us, length us, event | category | flops | bytes accessed | tf_op | source)
XLA Modules:
  0.0 102.1 jit_solution(672163295489945028)
XLA Ops:
  0.6 82.7 %fused_head.1 = (bf16[512,2560]{1,0:T(8,128)(2,1)}, f32[2560]{0:T(1024)}, f32[1,128]{1,0:T(1,128)}, bf16[512,4096]{1,0:T(8,128)(2,1)}, bf16[512,2560]{1,0:T(8,128)(2,1)}) custom-call(bf16[512,2560]{1,0:T(8,128)(2,1)} %refs_0_.1, f32[2560]{0:T(1024)} %refs_1_.1, bf16[4096,2560]{1,0:T(8,128)(2,1)} %refs_2_.1, s32[512,256]{1,0:T(8,128)} %refs_3_.1, ...), custom_call_target="tpu_custom_call" | custom-call | tf_op jit(solution)/shard_map/fused_head/pallas_call | solution.py:539
  83.3 18.6 %table_grad.1 = (f32[4096,2560]{1,0:T(8,128)}, bf16[512,2560]{1,0:T(8,128)(2,1)}, f32[2560]{0:T(1024)}, f32[1,128]{1,0:T(1,128)}) custom-call(bf16[512,4096]{1,0:T(8,128)(2,1)} %get-tuple-element.13.dz_hbm, bf16[512,2560]{1,0:T(8,128)(2,1)} %get-tuple-element.14.x_hbm, bf16[512,2560]{1,0:T(8,128)(2,1)} %get-tuple-element.15.dh_hbm, ...), custom_call_target="tpu_custom_call" | custom-call | tf_op jit(solution)/shard_map/table_grad/pallas_call | solution.py:589
